TPU v7x, 32 devices: a whole 2x2x4 slice. The times are simulated.
32 devices in a mesh: gx: 16 (over z, y, x), gy: 2 (over core).
Axes of the slice: x: 2, y: 2, z: 4, core: 2. Of those that a mesh axis runs over, the one named last changes fastest.
Arguments:
- bead_charge: float32 [16, 2, 16384], P('gx', 'gy'), may hold values from -6 to 6
- bead_cell: int32 [16, 2, 16384], P('gx', 'gy'), may hold values from 0 to 32767
- bead_count: int32 [16, 2], P('gx', 'gy'), may hold values from 8192 to 16384
- interp_weights: bfloat16 [16, 2, 12, 16384], P('gx', 'gy'), may hold values from 0.049804688 to 0.59765625
- kernel_fine: bfloat16 [17, 17, 17], replicated, may hold values from 0 to 4
- kernel_coarse: bfloat16 [17, 17, 17], replicated, may hold values from 0 to 4
Outputs:
- bead_potential: float32 [16, 2, 16384], P('gx', 'gy')
- potential_grid: float32 [256, 32, 128], P('gx', 'gy')
All inputs are finite; a program needn't handle non-finite values.
Results may differ from a plain program's by a relative error of at most 0.00076.
Values may be sent and summed in bfloat16 or wider, within the bound.
No kernel may reach another device: no remote copies, remote signals or barrier semaphores. Data moves between devices by JAX's collectives and lax.ppermute only.
A program may use at most 64 MiB of HBM per device.

v0:
```python
import jax
import jax.numpy as jnp
from jax import lax
from jax.experimental import pallas as pl
from jax.experimental.pallas import tpu as pltpu
from jax.sharding import PartitionSpec as P

LX = 16
LY = 16
LZ = 128
RADIUS = 8

SPAN = LX + 3
SPAN_PAD = 24
BLOCK = 2048
VMEM_BYTES = 24 * 1024 * 1024
REACH = 11
PLANES = SPAN + 2 * RADIUS
COLUMNS = 48
SHIFTS = RADIUS + 1
BANDS = 2 * RADIUS + 3
HALF = LZ // 2
KNOWN = 16
EDGE = 6
COARSE_OUT = 12
COARSE_IN = COARSE_OUT + 2 * RADIUS


def from_behind(value, axis, steps):
    count = lax.axis_size(axis)
    pairs = [(source, (source + steps) % count) for source in range(count)]
    return lax.ppermute(value, axis, pairs)


def hat_rows(rows, start, weights, period):
    places = lax.broadcasted_iota(jnp.int32, (rows, start.shape[1]), 0) - start
    if period:
        places = places & (period - 1)
    table = jnp.where(places == 3, weights[3:4], 0.0)
    for offset in (2, 1, 0):
        table = jnp.where(places == offset, weights[offset : offset + 1], table)
    return table


def bead_tables(cells, weights):
    first = hat_rows(SPAN_PAD, cells // (LY * LZ), weights[0:4], 0)
    second = hat_rows(SPAN_PAD, cells // LZ % LY, weights[4:8], 0)
    depth = hat_rows(LZ, cells % LZ, weights[8:12], LZ)
    return first, second, depth


def spread_kernel(count_ref, charge_ref, cell_ref, weight_ref, out_ref, up_ref, down_ref):
    step = pl.program_id(0)

    @pl.when(step == 0)
    def _():
        out_ref[...] = jnp.zeros_like(out_ref)

    cells = cell_ref[0]
    weights = weight_ref[0, 0].astype(jnp.float32)
    first, second, depth = bead_tables(cells, weights)
    slots = lax.broadcasted_iota(jnp.int32, cells.shape, 1) + step * BLOCK
    amount = jnp.where(slots < count_ref[0, 0], charge_ref[0], 0.0)
    first = first * amount
    face = jnp.concatenate([first[row : row + 1] * second for row in range(SPAN)], axis=0)
    high = face.astype(jnp.bfloat16)
    low = (face - high.astype(jnp.float32)).astype(jnp.bfloat16)
    depth = depth.astype(jnp.bfloat16)
    dims = (((1,), (1,)), ((), ()))
    out_ref[...] += lax.dot_general(
        high, depth, dims, preferred_element_type=jnp.float32
    ) + lax.dot_general(low, depth, dims, preferred_element_type=jnp.float32)

    @pl.when(step == pl.num_programs(0) - 1)
    def _():
        up_ref[...] = out_ref[(SPAN - REACH) * SPAN_PAD :].reshape(up_ref.shape)
        down_ref[...] = out_ref[: REACH * SPAN_PAD].reshape(down_ref.shape)


def read_kernel(count_ref, grid_ref, cell_ref, weight_ref, out_ref):
    step = pl.program_id(0)
    cells = cell_ref[0]
    weights = weight_ref[0, 0].astype(jnp.float32)
    first, second, depth = bead_tables(cells, weights)
    depth = depth.astype(jnp.bfloat16)
    along = jnp.dot(
        grid_ref[...],
        jnp.concatenate([depth, depth], axis=0),
        preferred_element_type=jnp.float32,
    )
    total = first[0:1] * along[0:SPAN_PAD]
    for row in range(1, SPAN):
        total = total + first[row : row + 1] * along[row * SPAN_PAD : (row + 1) * SPAN_PAD]
    picked = jnp.sum(total * second, axis=0, keepdims=True)
    slots = lax.broadcasted_iota(jnp.int32, cells.shape, 1) + step * BLOCK
    out_ref[0] = jnp.where(slots < count_ref[0, 0], picked, 0.0)


def bead_specs():
    row = pl.BlockSpec((1, 1, BLOCK), lambda i: (0, 0, i))
    weight = pl.BlockSpec((1, 1, 12, BLOCK), lambda i: (0, 0, 0, i))
    return pl.BlockSpec(memory_space=pltpu.SMEM), row, weight


def spread_beads(count, charge, cell, weights):
    scalar, row, weight = bead_specs()
    return pl.pallas_call(
        spread_kernel,
        grid=(charge.shape[2] // BLOCK,),
        in_specs=[scalar, row, row, weight],
        out_specs=(
            pl.BlockSpec((SPAN * SPAN_PAD, LZ), lambda i: (0, 0)),
            pl.BlockSpec((REACH, SPAN_PAD, LZ), lambda i: (0, 0, 0)),
            pl.BlockSpec((REACH, SPAN_PAD, LZ), lambda i: (0, 0, 0)),
        ),
        out_shape=(
            jax.ShapeDtypeStruct((SPAN * SPAN_PAD, LZ), jnp.float32),
            jax.ShapeDtypeStruct((REACH, SPAN_PAD, LZ), jnp.float32),
            jax.ShapeDtypeStruct((REACH, SPAN_PAD, LZ), jnp.float32),
        ),
        name="spread",
        compiler_params=pltpu.CompilerParams(vmem_limit_bytes=VMEM_BYTES),
    )(count, charge, cell, weights)


def read_beads(count, grid, cell, weights):
    scalar, row, weight = bead_specs()
    return pl.pallas_call(
        read_kernel,
        grid=(cell.shape[2] // BLOCK,),
        in_specs=[scalar, pl.BlockSpec(grid.shape, lambda i: (0, 0)), row, weight],
        out_specs=row,
        out_shape=jax.ShapeDtypeStruct(cell.shape, jnp.float32),
        name="read",
        compiler_params=pltpu.CompilerParams(vmem_limit_bytes=VMEM_BYTES),
    )(count, grid, cell, weights)


def spline_of(distance, period):
    place = (distance + 2) & (period - 1)
    return jnp.where(
        place == 2,
        0.75,
        jnp.where(
            (place == 1) | (place == 3), 0.5, jnp.where((place == 0) | (place == 4), 0.125, 0.0)
        ),
    )


PERIOD = 32


def tap_rows(taps):
    side = taps.shape[0]
    tap = lax.broadcasted_iota(jnp.int32, (side, LZ), 0)
    lane = lax.broadcasted_iota(jnp.int32, (side, LZ), 1)
    table = jnp.where(((lane + tap - RADIUS) & (PERIOD - 1)) == 0, 1.0, 0.0).astype(jnp.bfloat16)
    return jnp.dot(taps, table, preferred_element_type=jnp.float32)


def turned(row):
    return pltpu.roll(
        jnp.broadcast_to(row, (PERIOD, row.shape[1])), 0, 1, stride=1, stride_axis=0
    )


def near_mask(rows, depth):
    row = lax.broadcasted_iota(jnp.int32, (rows, LZ), 0)
    lane = lax.broadcasted_iota(jnp.int32, (rows, LZ), 1)
    near = ((row - lane + RADIUS) & (depth - 1)) <= 2 * RADIUS
    return jnp.where(near, 1.0, 0.0).astype(jnp.bfloat16)


def coarse_table_kernel(tap_ref, out_ref, row_ref):
    step = pl.program_id(0)
    lower_half = lax.broadcasted_iota(jnp.int32, (PERIOD, LZ), 1) < HALF
    mask = near_mask(HALF, HALF)
    row_ref[...] = jnp.zeros_like(row_ref)
    last = tap_ref.shape[0] - 1
    for side in range(2):
        plane = jnp.minimum(2 * step + side, last)
        weight = jnp.where(2 * step + side <= last, 1.0, 0.0)
        row_ref[1 : 2 + last] = tap_rows(tap_ref[plane]) * weight
        before = turned(row_ref[0:1])
        for band in range(BANDS - 1):
            after = turned(row_ref[band + 1 : band + 2])
            block = jnp.where(lower_half, after, before).astype(jnp.bfloat16)
            start = side * LZ + (band % 2) * HALF
            out_ref[0, band // 2, start : start + HALF] = (
                jnp.concatenate([block] * (HALF // PERIOD), axis=0) * mask
            )
            before = after


def coarse_table(kernel):
    pairs = (kernel.shape[0] + 1) // 2
    return pl.pallas_call(
        coarse_table_kernel,
        grid=(pairs,),
        in_specs=[pl.BlockSpec(kernel.shape, lambda i: (0, 0, 0))],
        out_specs=pl.BlockSpec((1, SHIFTS, 2 * LZ, LZ), lambda i: (i, 0, 0, 0)),
        out_shape=jax.ShapeDtypeStruct((pairs, SHIFTS, 2 * LZ, LZ), jnp.bfloat16),
        scratch_shapes=[pltpu.VMEM((SPAN_PAD, LZ), jnp.float32)],
        name="coarse_table",
        compiler_params=pltpu.CompilerParams(vmem_limit_bytes=VMEM_BYTES),
    )(kernel)


def three_terms(value):
    first = value.astype(jnp.bfloat16)
    rest = value - first.astype(jnp.float32)
    second = rest.astype(jnp.bfloat16)
    third = (rest - second.astype(jnp.float32)).astype(jnp.bfloat16)
    return first, second, third


def merged_plane(pieces, plane):
    own, below, above = pieces
    inner = plane - RADIUS
    if inner < 0:
        return below[plane]
    value = own[inner * SPAN_PAD : (inner + 1) * SPAN_PAD] if inner < SPAN else None
    if plane < REACH:
        return value + below[plane]
    if inner < LX:
        return value
    outer = above[inner - LX]
    return outer if value is None else value + outer


def gather_kernel(*refs):
    fine_ref, coarse_ref, up_ref, down_ref, half_ref = refs[-5:]
    own, before = refs[0:3], refs[3:6]
    after = before if len(refs) == 11 else refs[6:9]
    for plane in range(PLANES):
        middle = merged_plane(own, plane)
        lower = merged_plane(before, plane)
        upper = merged_plane(after, plane)
        value = jnp.concatenate(
            [
                lower[8:16],
                middle[0:8] + lower[16:24],
                middle[8:16],
                middle[16:24] + upper[0:8],
                upper[8:24],
            ],
            axis=0,
        )
        fine_ref[plane] = value.astype(jnp.bfloat16).astype(jnp.float32)
    spline = (0.125, 0.5, 0.75, 0.5, 0.125)
    for plane in range(KNOWN):
        total = spline[0] * fine_ref[2 * plane]
        for step in range(1, 5):
            total = total + spline[step] * fine_ref[2 * plane + step]
        half_ref[plane] = total
    total = spline[0] * half_ref[:, pl.ds(0, KNOWN, stride=2)]
    for step in range(1, 5):
        total = total + spline[step] * half_ref[:, pl.ds(step, KNOWN, stride=2)]
    terms = jnp.concatenate(three_terms(total.reshape(KNOWN * KNOWN, LZ)), axis=1)
    shape = (3 * LZ, LZ)
    fine_depth = lax.broadcasted_iota(jnp.int32, shape, 0) & (LZ - 1)
    coarse_depth = lax.broadcasted_iota(jnp.int32, shape, 1) & (HALF - 1)
    table = spline_of(fine_depth - 2 * coarse_depth, LZ).astype(jnp.bfloat16)
    coarse = jnp.dot(terms, table, preferred_element_type=jnp.float32)
    coarse = coarse.astype(jnp.bfloat16).reshape(coarse_ref.shape)
    coarse_ref[...] = coarse
    up_ref[...] = coarse[2 : 2 + EDGE]
    down_ref[...] = coarse[8 : 8 + EDGE]


def gather_fine(pieces):
    edge = jax.ShapeDtypeStruct((EDGE, KNOWN, LZ), jnp.bfloat16)
    return pl.pallas_call(
        gather_kernel,
        out_shape=(
            jax.ShapeDtypeStruct((PLANES, COLUMNS, LZ), jnp.float32),
            jax.ShapeDtypeStruct((KNOWN, KNOWN, LZ), jnp.bfloat16),
            edge,
            edge,
        ),
        scratch_shapes=[pltpu.VMEM((KNOWN, COLUMNS, LZ), jnp.float32)],
        name="gather",
        compiler_params=pltpu.CompilerParams(vmem_limit_bytes=VMEM_BYTES),
    )(*pieces)


def fine_kernel(fine_ref, tap_ref, out_ref, pair_ref, row_ref, even_ref, odd_ref):
    side = tap_ref.shape[0]
    row_ref[...] = jnp.zeros_like(row_ref)
    for plane in range(side):
        row_ref[plane, 1 : 1 + side] = tap_rows(tap_ref[plane])
    for shift in range(SHIFTS):
        halves = [fine_ref[:, pl.ds(2 * shift + part, 16, stride=2)] for part in range(2)]
        pair_ref[shift] = (
            jnp.concatenate(halves, axis=2).reshape(PLANES * 16, 2 * LZ).astype(jnp.bfloat16)
        )
    out_ref[...] = jnp.zeros_like(out_ref)

    def build(table_ref, plane):
        mask = near_mask(LZ, LZ)
        for band in range(BANDS):
            block = turned(row_ref[plane, band : band + 1]).astype(jnp.bfloat16)
            table_ref[band] = jnp.concatenate([block] * (LZ // PERIOD), axis=0) * mask

    def multiply(table_ref, plane):
        rows = pl.ds(pl.multiple_of(plane * 16, 16), SPAN * 16)
        total = out_ref[...]
        for shift in range(SHIFTS):
            band = 2 * shift + 1
            upper = jnp.concatenate([table_ref[band], table_ref[band - 1]], axis=1)
            lower = jnp.concatenate([table_ref[band + 1], table_ref[band]], axis=1)
            total = total + jnp.dot(
                pair_ref[shift, rows],
                jnp.concatenate([upper, lower], axis=0),
                preferred_element_type=jnp.float32,
            )
        out_ref[...] = total

    build(even_ref, 0)

    def two_planes(index, carry):
        plane = 2 * index
        build(odd_ref, plane + 1)
        multiply(even_ref, plane)
        build(even_ref, plane + 2)
        multiply(odd_ref, plane + 1)
        return carry

    lax.fori_loop(0, side // 2, two_planes, 0)
    multiply(even_ref, side - 1)


def fine_sums(fine, kernel):
    return pl.pallas_call(
        fine_kernel,
        out_shape=jax.ShapeDtypeStruct((SPAN * 16, 2 * LZ), jnp.float32),
        scratch_shapes=[
            pltpu.VMEM((SHIFTS, PLANES * 16, 2 * LZ), jnp.bfloat16),
            pltpu.VMEM((kernel.shape[0], SPAN_PAD, LZ), jnp.float32),
            pltpu.VMEM((BANDS, LZ, LZ), jnp.bfloat16),
            pltpu.VMEM((BANDS, LZ, LZ), jnp.bfloat16),
        ],
        name="fine",
        compiler_params=pltpu.CompilerParams(vmem_limit_bytes=VMEM_BYTES),
    )(fine, kernel)


def coarse_kernel(
    own_ref,
    below_ref,
    above_ref,
    low_ref,
    high_ref,
    table_ref,
    sums_ref,
    grid_ref,
    face_ref,
    cell_ref,
    pair_ref,
    total_ref,
    coarse_ref,
    wide_ref,
    join_ref,
):
    step = pl.program_id(0)

    @pl.when(step == 0)
    def _():
        total_ref[...] = jnp.zeros_like(total_ref)
        cell_ref[...] = jnp.zeros_like(cell_ref)
        for start, part in ((0, below_ref), (EDGE, own_ref), (EDGE + KNOWN, above_ref)):
            planes = slice(start, start + part.shape[0])
            values = part[...].astype(jnp.float32)
            cell_ref[planes, 8:24] = values
            if low_ref is None:
                cell_ref[planes, 0:8] = values[:, 8:16]
                cell_ref[planes, 24:32] = values[:, 0:8]
            else:
                cell_ref[planes, 0:8] = low_ref[planes].astype(jnp.float32)
                cell_ref[planes, 24:32] = high_ref[planes].astype(jnp.float32)
        lower_half = lax.broadcasted_iota(jnp.int32, (COARSE_IN + 1, 8, LZ), 2) < HALF
        for shift in range(SHIFTS):
            pair = jnp.where(
                lower_half,
                cell_ref[:, pl.ds(2 * shift + 2, 8, stride=2)],
                cell_ref[:, pl.ds(2 * shift + 3, 8, stride=2)],
            )
            rows = COARSE_IN * 8
            pair_ref[shift] = jnp.concatenate(
                [pair[:COARSE_IN].reshape(rows, LZ), pair[1:].reshape(rows, LZ)], axis=1
            ).astype(jnp.bfloat16)

    rows = pl.ds(pl.multiple_of(step * 16, 16), COARSE_OUT * 8)
    total = total_ref[...]
    for shift in range(SHIFTS):
        total = total + jnp.dot(
            pair_ref[shift, rows], table_ref[0, shift], preferred_element_type=jnp.float32
        )
    total_ref[...] = total

    @pl.when(step == pl.num_programs(0) - 1)
    def _():
        high = total.astype(jnp.bfloat16)
        low = (total - high.astype(jnp.float32)).astype(jnp.bfloat16)
        shape = (2 * LZ, 2 * LZ)
        source = lax.broadcasted_iota(jnp.int32, shape, 0)
        target = lax.broadcasted_iota(jnp.int32, shape, 1)
        table = jnp.where(
            (source // HALF) % 2 == target // LZ,
            spline_of((target & (LZ - 1)) - 2 * (source & (HALF - 1)), LZ),
            0.0,
        ).astype(jnp.bfloat16)
        deep = jnp.dot(
            jnp.concatenate([high, low], axis=1), table, preferred_element_type=jnp.float32
        )
        for part in range(2):
            coarse_ref[:, pl.ds(part, 8, stride=2)] = deep[:, part * LZ : (part + 1) * LZ].reshape(
                COARSE_OUT, 8, LZ
            )
        wide_ref[...] = jnp.zeros_like(wide_ref)
        for plane in range(SPAN):
            middle = plane // 2 + 1
            if plane % 2:
                value = (coarse_ref[middle] + coarse_ref[middle + 1]) * 0.5
            else:
                value = (
                    coarse_ref[middle - 1] + 6.0 * coarse_ref[middle] + coarse_ref[middle + 1]
                ) * 0.125
            wide_ref[plane, 0:16] = value
        before = wide_ref[:, 0:16]
        middle = wide_ref[:, 1:17]
        after = wide_ref[:, 2:18]
        even = (before + 6.0 * middle + after) * 0.125
        odd = (middle + after) * 0.5
        sums = sums_ref[...].reshape(SPAN, 16, 2 * LZ)
        join_ref[:, pl.ds(0, 16, stride=2)] = sums[:, :, :LZ] + even
        join_ref[:, pl.ds(1, 16, stride=2)] = sums[:, :, LZ:] + odd
        grid_ref[...] = join_ref[:LX, :LY]
        face = join_ref[:, :SPAN_PAD].reshape(SPAN * SPAN_PAD, LZ)
        face_high = face.astype(jnp.bfloat16)
        face_low = (face - face_high.astype(jnp.float32)).astype(jnp.bfloat16)
        face_ref[:, :LZ] = face_high
        face_ref[:, LZ:] = face_low


def potentials(own, below, above, low, high, table, sums):
    def whole(value):
        return pl.BlockSpec(value.shape, lambda i: (0,) * value.ndim)

    given = [own, below, above] + ([] if low is None else [low, high])
    specs = [whole(value) for value in given]
    specs.append(pl.BlockSpec((1, SHIFTS, 2 * LZ, LZ), lambda i: (i, 0, 0, 0)))
    specs.append(whole(sums))

    def body(*refs):
        if low is None:
            refs = refs[:3] + (None, None) + refs[3:]
        coarse_kernel(*refs)

    return pl.pallas_call(
        body,
        grid=(table.shape[0],),
        in_specs=specs,
        out_specs=(
            pl.BlockSpec((LX, LY, LZ), lambda i: (0, 0, 0)),
            pl.BlockSpec((SPAN * SPAN_PAD, 2 * LZ), lambda i: (0, 0)),
        ),
        out_shape=(
            jax.ShapeDtypeStruct((LX, LY, LZ), jnp.float32),
            jax.ShapeDtypeStruct((SPAN * SPAN_PAD, 2 * LZ), jnp.bfloat16),
        ),
        scratch_shapes=[
            pltpu.VMEM((COARSE_IN + 1, 40, LZ), jnp.float32),
            pltpu.VMEM((SHIFTS, COARSE_IN * 8, 2 * LZ), jnp.bfloat16),
            pltpu.VMEM((COARSE_OUT * 8, LZ), jnp.float32),
            pltpu.VMEM((COARSE_OUT, 16, LZ), jnp.float32),
            pltpu.VMEM((SPAN, 24, LZ), jnp.float32),
            pltpu.VMEM((SPAN, 32, LZ), jnp.float32),
        ],
        name="coarse",
        compiler_params=pltpu.CompilerParams(vmem_limit_bytes=VMEM_BYTES),
    )(*given, table, sums)


def on_device(bead_charge, bead_cell, bead_count, interp_weights, kernel_fine, kernel_coarse):
    own, up, down = spread_beads(bead_count, bead_charge, bead_cell, interp_weights)
    below = from_behind(up, "gx", 1)
    above = from_behind(down, "gx", -1)
    table_coarse = coarse_table(kernel_coarse)
    wraps = lax.axis_size("gy") == 2
    pieces = [own, below, above]
    for steps in (1,) if wraps else (1, -1):
        pieces += [from_behind(part, "gy", steps) for part in (own, below, above)]
    fine, coarse, coarse_up, coarse_down = gather_fine(pieces)
    coarse_below = from_behind(coarse_up, "gx", 1)
    coarse_above = from_behind(coarse_down, "gx", -1)
    sums = fine_sums(fine, kernel_fine)
    low = high = None
    if not wraps:
        joined = jnp.concatenate([coarse_below, coarse, coarse_above], axis=0)
        low = from_behind(joined[:, :8], "gy", 1)
        high = from_behind(joined[:, 8:], "gy", -1)
    potential_grid, face = potentials(
        coarse, coarse_below, coarse_above, low, high, table_coarse, sums
    )
    bead_potential = read_beads(bead_count, face, bead_cell, interp_weights)
    return (bead_potential, potential_grid)


def solution(mesh):
    return jax.shard_map(
        on_device,
        mesh=mesh,
        in_specs=(
            P("gx", "gy", None),
            P("gx", "gy", None),
            P("gx", "gy"),
            P("gx", "gy", None, None),
            P(),
            P(),
        ),
        out_specs=(P("gx", "gy", None), P("gx", "gy", None)),
        check_vma=False,
    )
```

profile of v0, /device:TPU:0, one launch (start us, length us, event | category | flops | bytes accessed | tf_op | source)
XLA Modules:
  0.0 63.4 jit_solution(5402803807162798477)
XLA Ops:
  1.3 0.0 copy-start
  1.3 1.0 %copy-done = bf16[1,1,12,16384]{3,2,1,0:T(8,128)(2,1)S(1)} copy-done((bf16[1,1,12,16384]{3,2,1,0:T(8,128)(2,1)S(1)}, bf16[1,1,12,16384]{3,2,1,0:T(8,128)(2,1)}, u32[]{:S(2)}) %copy-start) | copy-done | bytes 393240
  2.3 0.0 copy-start.2
  2.3 0.8 %copy-done.2 = s32[1,1,16384]{2,1,0:T(1,128)S(1)} copy-done((s32[1,1,16384]{2,1,0:T(1,128)S(1)}, s32[1,1,16384]{2,1,0:T(1,128)}, u32[]{:S(2)}) %copy-start.2) | copy-done | bytes 65560
  3.2 0.0 copy-start.6
  3.2 0.8 %copy-done.6 = f32[1,1,16384]{2,1,0:T(1,128)S(1)} copy-done((f32[1,1,16384]{2,1,0:T(1,128)S(1)}, f32[1,1,16384]{2,1,0:T(1,128)}, u32[]{:S(2)}) %copy-start.6) | copy-done | bytes 65560
  4.0 0.0 copy-start.4
  4.0 15.8 %spread.1 = (f32[456,128]{1,0:T(8,128)S(1)}, f32[11,24,128]{2,1,0:T(8,128)S(1)}, f32[11,24,128]{2,1,0:T(8,128)S(1)}) custom-call(s32[1,1]{1,0:T(1,128)S(6)} %copy.8.count_ref, f32[1,1,16384]{2,1,0:T(1,128)S(1)} %copy-done.6, s32[1,1,16384]{2,1,0:T(1,128)S(1)} %copy-done.2, bf16[1,1,12,16384]{3,2,1,0:T(8,128)(2,1)S(1)} %copy-done), custom_call_target="tpu_custom_call" | custom-call | tf_op jit(solution)/shard_map/spread/pallas_call | solution.py:107
  19.8 3.0 %collective-permute-start = (f32[11,24,128]{2,1,0:T(8,128)S(1)}, f32[11,24,128]{2,1,0:T(8,128)S(1)}, u32[]{:S(2)}, u32[]{:S(2)}) collective-permute-start(f32[11,24,128]{2,1,0:T(8,128)S(1)} %get-tuple-element.12), channel_id=1, source_target_pairs={{0,2},{2,4},{4,6},{6,8},{8,10},{10,12},{12,14},{14,16},{16,18},{18... | collective-permute-start | bytes 405512 | tf_op jit(solution)/shard_map/ppermute | solution.py:32
  22.8 4.1 %collective-permute-start.1 = (f32[11,24,128]{2,1,0:T(8,128)S(1)}, f32[11,24,128]{2,1,0:T(8,128)S(1)}, u32[]{:S(2)}, u32[]{:S(2)}) collective-permute-start(f32[11,24,128]{2,1,0:T(8,128)S(1)} %get-tuple-element.13), channel_id=1, source_target_pairs={{0,30},{2,0},{4,2},{6,4},{8,6},{10,8},{12,10},{14,12},{16,14},{18,... | collective-permute-start | bytes 405512 | tf_op jit(solution)/shard_map/ppermute | solution.py:32
  26.9 0.0 collective-permute-start.2
  26.9 3.6 %collective-permute-done.refs_1_ = f32[11,24,128]{2,1,0:T(8,128)S(1)} collective-permute-done((f32[11,24,128]{2,1,0:T(8,128)S(1)}, f32[11,24,128]{2,1,0:T(8,128)S(1)}, u32[]{:S(2)}, u32[]{:S(2)}) %collective-permute-start) | collective-permute-done | bytes 135200 | tf_op jit(solution)/shard_map/ppermute | solution.py:32
  30.5 0.0 collective-permute-start.3
  30.5 0.0 collective-permute-done.1.refs_2_
  30.5 0.5 collective-permute-start.4
  31.0 0.0 collective-permute-done.2.refs_3_
  31.0 0.8 %collective-permute-done.3.refs_4_ = f32[11,24,128]{2,1,0:T(8,128)S(1)} collective-permute-done((f32[11,24,128]{2,1,0:T(8,128)S(1)}, f32[11,24,128]{2,1,0:T(8,128)S(1)}, u32[]{:S(2)}, u32[]{:S(2)}) %collective-permute-start.3) | collective-permute-done | bytes 135200 | tf_op jit(solution)/shard_map/ppermute | solution.py:32
  31.9 0.2 collective-permute-done.4.refs_5_
  32.1 0.5 gather.1
  32.5 1.4 %collective-permute-start.5 = (bf16[6,16,128]{2,1,0:T(8,128)(2,1)S(1)}, bf16[6,16,128]{2,1,0:T(8,128)(2,1)S(1)}, u32[]{:S(2)}, u32[]{:S(2)}) collective-permute-start(bf16[6,16,128]{2,1,0:T(8,128)(2,1)S(1)} %get-tuple-element.15), channel_id=1, source_target_pairs={{0,2},{2,4},{4,6},{6,8},{8,10},{10,12},{12,14},{14,16},{16,18},{18... | collective-permute-start | bytes 73736 | tf_op jit(solution)/shard_map/ppermute | solution.py:32
  33.9 0.0 copy-start.1
  33.9 0.0 copy-start.3
  33.9 4.3 %collective-permute-start.6 = (bf16[6,16,128]{2,1,0:T(8,128)(2,1)S(1)}, bf16[6,16,128]{2,1,0:T(8,128)(2,1)S(1)}, u32[]{:S(2)}, u32[]{:S(2)}) collective-permute-start(bf16[6,16,128]{2,1,0:T(8,128)(2,1)S(1)} %get-tuple-element.16), channel_id=1, source_target_pairs={{0,30},{2,0},{4,2},{6,4},{8,6},{10,8},{12,10},{14,12},{16,14},{18,... | collective-permute-start | bytes 73736 | tf_op jit(solution)/shard_map/ppermute | solution.py:32
  38.2 0.0 copy-start.5
  38.2 0.9 %copy-done.5 = bf16[17,17,17]{2,1,0:T(8,128)(2,1)S(1)} copy-done((bf16[17,17,17]{2,1,0:T(8,128)(2,1)S(1)}, bf16[17,17,17]{2,1,0:T(8,128)(2,1)}, u32[]{:S(2)}) %copy-start.5) | copy-done | bytes 9850
  39.1 2.9 %coarse_table.1.refs_3_ = bf16[9,9,256,128]{3,2,1,0:T(8,128)(2,1)S(1)} custom-call(bf16[17,17,17]{2,1,0:T(8,128)(2,1)S(1)} %copy-done.5), custom_call_target="tpu_custom_call" | custom-call | tf_op jit(solution)/shard_map/coarse_table/pallas_call | solution.py:197
  42.0 0.0 copy-done.4
  42.0 9.1 %fine.1.refs_4_ = f32[304,256]{1,0:T(8,128)S(1)} custom-call(f32[35,48,128]{2,1,0:T(8,128)S(1)} %get-tuple-element.17.fine_ref, bf16[17,17,17]{2,1,0:T(8,128)(2,1)S(1)} %copy-done.4), custom_call_target="tpu_custom_call" | custom-call | tf_op jit(solution)/shard_map/fine/pallas_call | solution.py:334
  51.2 0.0 collective-permute-done.5.refs_1_
  51.2 0.0 collective-permute-done.6.refs_2_
  51.2 3.8 %coarse.1 = (f32[16,16,128]{2,1,0:T(8,128)}, bf16[456,256]{1,0:T(8,128)(2,1)S(1)}) custom-call(bf16[16,16,128]{2,1,0:T(8,128)(2,1)S(1)} %get-tuple-element.14.refs_0_, bf16[6,16,128]{2,1,0:T(8,128)(2,1)S(1)} %collective-permute-done.5.refs_1_, bf16[6,16,128]{2,1,0:T(8,128)(2,1)S(1)} %collective-permute-done.6.refs_2_, ...), custom_call_target="tpu_custom_call" | custom-call | tf_op jit(solution)/shard_map/coarse/pallas_call | solution.py:460
  55.0 0.0 copy-done.1
  55.0 0.0 copy-done.3
  55.0 8.4 %read.1 = f32[1,1,16384]{2,1,0:T(1,128)} custom-call(s32[1,1]{1,0:T(1,128)S(6)} %copy.8.count_ref, bf16[456,256]{1,0:T(8,128)(2,1)S(1)} %get-tuple-element.18.grid_ref, s32[1,1,16384]{2,1,0:T(1,128)S(1)} %copy-done.3, bf16[1,1,12,16384]{3,2,1,0:T(8,128)(2,1)S(1)} %copy-done.1), custom_call_target="tpu_custom_call" | custom-call | tf_op jit(solution)/shard_map/read/pallas_call | solution.py:128
Async XLA Ops:
  1.3 1.0 %copy-start = (bf16[1,1,12,16384]{3,2,1,0:T(8,128)(2,1)S(1)}, bf16[1,1,12,16384]{3,2,1,0:T(8,128)(2,1)}, u32[]{:S(2)}) copy-start(bf16[1,1,12,16384]{3,2,1,0:T(8,128)(2,1)} %weight_ref.3) | copy-start | bytes 1179652
  2.3 0.8 %copy-start.2 = (s32[1,1,16384]{2,1,0:T(1,128)S(1)}, s32[1,1,16384]{2,1,0:T(1,128)}, u32[]{:S(2)}) copy-start(s32[1,1,16384]{2,1,0:T(1,128)} %cell_ref.3) | copy-start | bytes 196612
  3.2 0.8 %copy-start.6 = (f32[1,1,16384]{2,1,0:T(1,128)S(1)}, f32[1,1,16384]{2,1,0:T(1,128)}, u32[]{:S(2)}) copy-start(f32[1,1,16384]{2,1,0:T(1,128)} %charge_ref.1) | copy-start | bytes 196612
  4.0 38.0 %copy-start.4 = (bf16[17,17,17]{2,1,0:T(8,128)(2,1)S(1)}, bf16[17,17,17]{2,1,0:T(8,128)(2,1)}, u32[]{:S(2)}) copy-start(bf16[17,17,17]{2,1,0:T(8,128)(2,1)} %tap_ref.3) | copy-start | bytes 29482
  19.8 10.7 %collective-permute-start = (f32[11,24,128]{2,1,0:T(8,128)S(1)}, f32[11,24,128]{2,1,0:T(8,128)S(1)}, u32[]{:S(2)}, u32[]{:S(2)}) collective-permute-start(f32[11,24,128]{2,1,0:T(8,128)S(1)} %get-tuple-element.12), channel_id=1, source_target_pairs={{0,2},{2,4},{4,6},{6,8},{8,10},{10,12},{12,14},{14,16},{16,18},{18... | collective-permute-start | bytes 405512 | tf_op jit(solution)/shard_map/ppermute | solution.py:32
  22.8 7.7 %collective-permute-start.1 = (f32[11,24,128]{2,1,0:T(8,128)S(1)}, f32[11,24,128]{2,1,0:T(8,128)S(1)}, u32[]{:S(2)}, u32[]{:S(2)}) collective-permute-start(f32[11,24,128]{2,1,0:T(8,128)S(1)} %get-tuple-element.13), channel_id=1, source_target_pairs={{0,30},{2,0},{4,2},{6,4},{8,6},{10,8},{12,10},{14,12},{16,14},{18,... | collective-permute-start | bytes 405512 | tf_op jit(solution)/shard_map/ppermute | solution.py:32
  26.9 4.1 %collective-permute-start.2 = (f32[456,128]{1,0:T(8,128)S(1)}, f32[456,128]{1,0:T(8,128)S(1)}, u32[]{:S(2)}, u32[]{:S(2)}) collective-permute-start(f32[456,128]{1,0:T(8,128)S(1)} %get-tuple-element.11.refs_0_), channel_id=1, source_target_pairs={{0,1},{1,0},{2,3},{3,2},{4,5},{5,4},{6,7},{7,6},{8,9},{9,8},{10,11... | collective-permute-start | bytes 700424 | tf_op jit(solution)/shard_map/ppermute | solution.py:32
  30.5 1.4 %collective-permute-start.3 = (f32[11,24,128]{2,1,0:T(8,128)S(1)}, f32[11,24,128]{2,1,0:T(8,128)S(1)}, u32[]{:S(2)}, u32[]{:S(2)}) collective-permute-start(f32[11,24,128]{2,1,0:T(8,128)S(1)} %collective-permute-done.refs_1_), channel_id=1, source_target_pairs={{0,1},{1,0},{2,3},{3,2},{4,5},{5,4},{6,7},{7,6},{8,9},{9,8},{10,11... | collective-permute-start | bytes 405512 | tf_op jit(solution)/shard_map/ppermute | solution.py:32
  30.5 1.5 %collective-permute-start.4 = (f32[11,24,128]{2,1,0:T(8,128)S(1)}, f32[11,24,128]{2,1,0:T(8,128)S(1)}, u32[]{:S(2)}, u32[]{:S(2)}) collective-permute-start(f32[11,24,128]{2,1,0:T(8,128)S(1)} %collective-permute-done.1.refs_2_), channel_id=1, source_target_pairs={{0,1},{1,0},{2,3},{3,2},{4,5},{5,4},{6,7},{7,6},{8,9},{9,8},{10,11... | collective-permute-start | bytes 405512 | tf_op jit(solution)/shard_map/ppermute | solution.py:32
  32.5 18.6 %collective-permute-start.5 = (bf16[6,16,128]{2,1,0:T(8,128)(2,1)S(1)}, bf16[6,16,128]{2,1,0:T(8,128)(2,1)S(1)}, u32[]{:S(2)}, u32[]{:S(2)}) collective-permute-start(bf16[6,16,128]{2,1,0:T(8,128)(2,1)S(1)} %get-tuple-element.15), channel_id=1, source_target_pairs={{0,2},{2,4},{4,6},{6,8},{8,10},{10,12},{12,14},{14,16},{16,18},{18... | collective-permute-start | bytes 73736 | tf_op jit(solution)/shard_map/ppermute | solution.py:32
  33.9 21.1 %copy-start.1 = (bf16[1,1,12,16384]{3,2,1,0:T(8,128)(2,1)S(1)}, bf16[1,1,12,16384]{3,2,1,0:T(8,128)(2,1)}, u32[]{:S(2)}) copy-start(bf16[1,1,12,16384]{3,2,1,0:T(8,128)(2,1)} %weight_ref.3) | copy-start | bytes 1179652
  33.9 21.1 %copy-start.3 = (s32[1,1,16384]{2,1,0:T(1,128)S(1)}, s32[1,1,16384]{2,1,0:T(1,128)}, u32[]{:S(2)}) copy-start(s32[1,1,16384]{2,1,0:T(1,128)} %cell_ref.3) | copy-start | bytes 196612
  33.9 17.3 %collective-permute-start.6 = (bf16[6,16,128]{2,1,0:T(8,128)(2,1)S(1)}, bf16[6,16,128]{2,1,0:T(8,128)(2,1)S(1)}, u32[]{:S(2)}, u32[]{:S(2)}) collective-permute-start(bf16[6,16,128]{2,1,0:T(8,128)(2,1)S(1)} %get-tuple-element.16), channel_id=1, source_target_pairs={{0,30},{2,0},{4,2},{6,4},{8,6},{10,8},{12,10},{14,12},{16,14},{18,... | collective-permute-start | bytes 73736 | tf_op jit(solution)/shard_map/ppermute | solution.py:32
  38.2 0.9 %copy-start.5 = (bf16[17,17,17]{2,1,0:T(8,128)(2,1)S(1)}, bf16[17,17,17]{2,1,0:T(8,128)(2,1)}, u32[]{:S(2)}) copy-start(bf16[17,17,17]{2,1,0:T(8,128)(2,1)} %tap_ref.2) | copy-start | bytes 29482
where the time goes:
time: 63.7 us; the launch traced here: 63.4 us
  Pallas kernels  40.6 us (64%)
  starting transfers between devices  13.3 us (21%)
  waiting for transfers between devices  4.64 us (7%)
  local copies, waits for them, and re-layouts  3.62 us (6%)
  between operations  1.35 us (2%)
    pallas_call x1, Pallas kernels, spread_beads(): pl.pallas_call(spread_kernel, grid=(charge.shape[2] // BLOCK,), in_specs=...  15.8 us
    ppermute x7, starting transfers between devices, from_behind(): return lax.ppermute(value, axis, pairs)  13.3 us
    pallas_call x1, Pallas kernels, fine_sums(): pl.pallas_call(fine_kernel, out_shape=jax.ShapeDtypeStruct((SPAN * 16, 2...  9.13 us
    pallas_call x1, Pallas kernels, read_beads(): pl.pallas_call(read_kernel, grid=(cell.shape[2] // BLOCK,), in_specs=[sca...  8.42 us
    ppermute x7, waiting for transfers between devices, from_behind(): return lax.ppermute(value, axis, pairs)  4.64 us
    pallas_call x1, Pallas kernels, potentials(): pl.pallas_call(body, grid=(table.shape[0],), in_specs=specs, out_specs=(p...  3.85 us
    unnamed x14, local copies, waits for them, and re-layouts  3.62 us
    pallas_call x1, Pallas kernels, coarse_table(): pl.pallas_call(coarse_table_kernel, grid=(pairs,), in_specs=[pl.BlockSpec...  2.89 us
  transfers between devices with their start and end apart: 7, of which 3 were waited for; matrix products, arithmetic and copies ran while one was open for 0% of the time, Pallas kernels for 19%

commit v1 on v0

--- a/solution.py
+++ b/solution.py
@@ -13,6 +13,9 @@
 SPAN = LX + 3
 SPAN_PAD = 24
 BLOCK = 2048
+CHUNK = 256
+READ_CHUNK = 512
+FACE = SPAN * LY + (SPAN - LY) * SPAN_PAD
 VMEM_BYTES = 24 * 1024 * 1024
 REACH = 11
 PLANES = SPAN + 2 * RADIUS
@@ -42,98 +45,166 @@
     return table
 
 
+def depth_rows(start, weights):
+    groups = LZ // 8
+    pattern = hat_rows(16, start & 7, weights, 0)
+    low, high = pattern[:8], pattern[8:]
+    group = jnp.broadcast_to(start // 8, low.shape)
+    here = [group == place for place in range(groups)]
+    rows = [
+        jnp.where(here[place], low, jnp.where(here[place - 1], high, 0.0))
+        for place in range(groups)
+    ]
+    return jnp.concatenate(rows, axis=0)
+
+
 def bead_tables(cells, weights):
     first = hat_rows(SPAN_PAD, cells // (LY * LZ), weights[0:4], 0)
     second = hat_rows(SPAN_PAD, cells // LZ % LY, weights[4:8], 0)
-    depth = hat_rows(LZ, cells % LZ, weights[8:12], LZ)
+    depth = depth_rows(cells % LZ, weights[8:12])
     return first, second, depth
 
 
-def spread_kernel(count_ref, charge_ref, cell_ref, weight_ref, out_ref, up_ref, down_ref):
+def face_rows(first, second):
+    inside = [first[row : row + 1] * second[:LY] for row in range(SPAN)]
+    outside = [second[row : row + 1] * first for row in range(LY, SPAN)]
+    return jnp.concatenate(inside + outside, axis=0)
+
+
+def spread_kernel(
+    count_ref,
+    charge_ref,
+    cell_ref,
+    weight_ref,
+    out_ref,
+    up_ref,
+    down_ref,
+    depth_ref,
+    first_ref,
+    second_ref,
+    total_ref,
+    order_ref,
+):
     step = pl.program_id(0)
 
     @pl.when(step == 0)
     def _():
-        out_ref[...] = jnp.zeros_like(out_ref)
-
-    cells = cell_ref[0]
-    weights = weight_ref[0, 0].astype(jnp.float32)
-    first, second, depth = bead_tables(cells, weights)
-    slots = lax.broadcasted_iota(jnp.int32, cells.shape, 1) + step * BLOCK
-    amount = jnp.where(slots < count_ref[0, 0], charge_ref[0], 0.0)
-    first = first * amount
-    face = jnp.concatenate([first[row : row + 1] * second for row in range(SPAN)], axis=0)
-    high = face.astype(jnp.bfloat16)
-    low = (face - high.astype(jnp.float32)).astype(jnp.bfloat16)
-    depth = depth.astype(jnp.bfloat16)
+        total_ref[...] = jnp.zeros_like(total_ref)
+
     dims = (((1,), (1,)), ((), ()))
-    out_ref[...] += lax.dot_general(
-        high, depth, dims, preferred_element_type=jnp.float32
-    ) + lax.dot_general(low, depth, dims, preferred_element_type=jnp.float32)
+    total = None
+    for start in range(0, BLOCK, CHUNK):
+        beads = slice(start, start + CHUNK)
+        cells = cell_ref[0, :, beads]
+        weights = weight_ref[0, 0, :, beads].astype(jnp.float32)
+        first, second, depth = bead_tables(cells, weights)
+        depth = depth.astype(jnp.bfloat16)
+        depth_ref[:, beads] = depth
+        first_ref[:, beads] = first
+        second_ref[:, beads] = second
+        slots = lax.broadcasted_iota(jnp.int32, cells.shape, 1) + (step * BLOCK + start)
+        amount = jnp.where(slots < count_ref[0, 0], charge_ref[0, :, beads], 0.0)
+        face = face_rows(first * amount, second)
+        high = face.astype(jnp.bfloat16)
+        low = (face - high.astype(jnp.float32)).astype(jnp.bfloat16)
+        for term in (high, low):
+            part = lax.dot_general(term, depth, dims, preferred_element_type=jnp.float32)
+            total = part if total is None else total + part
+    total_ref[...] += total
 
     @pl.when(step == pl.num_programs(0) - 1)
     def _():
-        up_ref[...] = out_ref[(SPAN - REACH) * SPAN_PAD :].reshape(up_ref.shape)
-        down_ref[...] = out_ref[: REACH * SPAN_PAD].reshape(down_ref.shape)
-
-
-def read_kernel(count_ref, grid_ref, cell_ref, weight_ref, out_ref):
+        order_ref[...] = jnp.zeros_like(order_ref)
+        for plane in range(SPAN):
+            order_ref[plane * SPAN_PAD : plane * SPAN_PAD + LY] = total_ref[
+                plane * LY : (plane + 1) * LY
+            ]
+        for column in range(SPAN - LY):
+            start = SPAN * LY + column * SPAN_PAD
+            order_ref[pl.ds(LY + column, SPAN_PAD, stride=SPAN_PAD)] = total_ref[
+                start : start + SPAN_PAD
+            ]
+        out_ref[...] = order_ref[: SPAN * SPAN_PAD]
+        up_ref[...] = order_ref[(SPAN - REACH) * SPAN_PAD : SPAN * SPAN_PAD].reshape(up_ref.shape)
+        down_ref[...] = order_ref[: REACH * SPAN_PAD].reshape(down_ref.shape)
+
+
+def read_kernel(count_ref, grid_ref, depth_ref, first_ref, second_ref, out_ref):
     step = pl.program_id(0)
-    cells = cell_ref[0]
-    weights = weight_ref[0, 0].astype(jnp.float32)
-    first, second, depth = bead_tables(cells, weights)
-    depth = depth.astype(jnp.bfloat16)
-    along = jnp.dot(
-        grid_ref[...],
-        jnp.concatenate([depth, depth], axis=0),
-        preferred_element_type=jnp.float32,
-    )
-    total = first[0:1] * along[0:SPAN_PAD]
-    for row in range(1, SPAN):
-        total = total + first[row : row + 1] * along[row * SPAN_PAD : (row + 1) * SPAN_PAD]
-    picked = jnp.sum(total * second, axis=0, keepdims=True)
-    slots = lax.broadcasted_iota(jnp.int32, cells.shape, 1) + step * BLOCK
-    out_ref[0] = jnp.where(slots < count_ref[0, 0], picked, 0.0)
-
-
-def bead_specs():
+    for start in range(0, BLOCK, READ_CHUNK):
+        beads = slice(start, start + READ_CHUNK)
+        depth = depth_ref[:, beads]
+        along = jnp.dot(
+            grid_ref[...],
+            jnp.concatenate([depth, depth], axis=0),
+            preferred_element_type=jnp.float32,
+        )
+        first = first_ref[:, beads]
+        second = second_ref[:, beads]
+        inside = first[0:1] * along[0:LY]
+        for row in range(1, SPAN):
+            inside = inside + first[row : row + 1] * along[row * LY : (row + 1) * LY]
+        inside = inside * second[:LY]
+        outside = None
+        for column in range(SPAN - LY):
+            place = SPAN * LY + column * SPAN_PAD
+            part = second[LY + column : LY + column + 1] * along[place : place + SPAN_PAD]
+            outside = part if outside is None else outside + part
+        outside = outside * first
+        parts = [inside[row : row + 8] for row in range(0, LY, 8)]
+        parts += [outside[row : row + 8] for row in range(0, SPAN_PAD, 8)]
+        picked = jnp.sum(sum(parts[1:], parts[0]), axis=0, keepdims=True)
+        slots = lax.broadcasted_iota(jnp.int32, picked.shape, 1) + (step * BLOCK + start)
+        out_ref[0, :, beads] = jnp.where(slots < count_ref[0, 0], picked, 0.0)
+
+
+def whole_spec(shape):
+    return pl.BlockSpec(shape, lambda i: (0,) * len(shape))
+
+
+def table_specs():
+    return [pl.BlockSpec((rows, BLOCK), lambda i: (0, i)) for rows in (LZ, SPAN_PAD, SPAN_PAD)]
+
+
+def spread_beads(count, charge, cell, weights):
+    slots = charge.shape[2]
     row = pl.BlockSpec((1, 1, BLOCK), lambda i: (0, 0, i))
     weight = pl.BlockSpec((1, 1, 12, BLOCK), lambda i: (0, 0, 0, i))
-    return pl.BlockSpec(memory_space=pltpu.SMEM), row, weight
-
-
-def spread_beads(count, charge, cell, weights):
-    scalar, row, weight = bead_specs()
+    edge = (REACH, SPAN_PAD, LZ)
+    shapes = [
+        jax.ShapeDtypeStruct((SPAN * SPAN_PAD, LZ), jnp.float32),
+        jax.ShapeDtypeStruct(edge, jnp.float32),
+        jax.ShapeDtypeStruct(edge, jnp.float32),
+        jax.ShapeDtypeStruct((LZ, slots), jnp.bfloat16),
+        jax.ShapeDtypeStruct((SPAN_PAD, slots), jnp.float32),
+        jax.ShapeDtypeStruct((SPAN_PAD, slots), jnp.float32),
+    ]
     return pl.pallas_call(
         spread_kernel,
-        grid=(charge.shape[2] // BLOCK,),
-        in_specs=[scalar, row, row, weight],
-        out_specs=(
-            pl.BlockSpec((SPAN * SPAN_PAD, LZ), lambda i: (0, 0)),
-            pl.BlockSpec((REACH, SPAN_PAD, LZ), lambda i: (0, 0, 0)),
-            pl.BlockSpec((REACH, SPAN_PAD, LZ), lambda i: (0, 0, 0)),
-        ),
-        out_shape=(
-            jax.ShapeDtypeStruct((SPAN * SPAN_PAD, LZ), jnp.float32),
-            jax.ShapeDtypeStruct((REACH, SPAN_PAD, LZ), jnp.float32),
-            jax.ShapeDtypeStruct((REACH, SPAN_PAD, LZ), jnp.float32),
-        ),
+        grid=(slots // BLOCK,),
+        in_specs=[pl.BlockSpec(memory_space=pltpu.SMEM), row, row, weight],
+        out_specs=[whole_spec(part.shape) for part in shapes[:3]] + table_specs(),
+        out_shape=shapes,
+        scratch_shapes=[
+            pltpu.VMEM((FACE, LZ), jnp.float32),
+            pltpu.VMEM((SPAN_PAD * SPAN_PAD, LZ), jnp.float32),
+        ],
         name="spread",
         compiler_params=pltpu.CompilerParams(vmem_limit_bytes=VMEM_BYTES),
     )(count, charge, cell, weights)
 
 
-def read_beads(count, grid, cell, weights):
-    scalar, row, weight = bead_specs()
+def read_beads(count, grid, tables):
+    slots = tables[0].shape[1]
     return pl.pallas_call(
         read_kernel,
-        grid=(cell.shape[2] // BLOCK,),
-        in_specs=[scalar, pl.BlockSpec(grid.shape, lambda i: (0, 0)), row, weight],
-        out_specs=row,
-        out_shape=jax.ShapeDtypeStruct(cell.shape, jnp.float32),
+        grid=(slots // BLOCK,),
+        in_specs=[pl.BlockSpec(memory_space=pltpu.SMEM), whole_spec(grid.shape)] + table_specs(),
+        out_specs=pl.BlockSpec((1, 1, BLOCK), lambda i: (0, 0, i)),
+        out_shape=jax.ShapeDtypeStruct((1, 1, slots), jnp.float32),
         name="read",
         compiler_params=pltpu.CompilerParams(vmem_limit_bytes=VMEM_BYTES),
-    )(count, grid, cell, weights)
+    )(count, grid, *tables)
 
 
 def spline_of(distance, period):
@@ -169,41 +240,6 @@
     lane = lax.broadcasted_iota(jnp.int32, (rows, LZ), 1)
     near = ((row - lane + RADIUS) & (depth - 1)) <= 2 * RADIUS
     return jnp.where(near, 1.0, 0.0).astype(jnp.bfloat16)
-
-
-def coarse_table_kernel(tap_ref, out_ref, row_ref):
-    step = pl.program_id(0)
-    lower_half = lax.broadcasted_iota(jnp.int32, (PERIOD, LZ), 1) < HALF
-    mask = near_mask(HALF, HALF)
-    row_ref[...] = jnp.zeros_like(row_ref)
-    last = tap_ref.shape[0] - 1
-    for side in range(2):
-        plane = jnp.minimum(2 * step + side, last)
-        weight = jnp.where(2 * step + side <= last, 1.0, 0.0)
-        row_ref[1 : 2 + last] = tap_rows(tap_ref[plane]) * weight
-        before = turned(row_ref[0:1])
-        for band in range(BANDS - 1):
-            after = turned(row_ref[band + 1 : band + 2])
-            block = jnp.where(lower_half, after, before).astype(jnp.bfloat16)
-            start = side * LZ + (band % 2) * HALF
-            out_ref[0, band // 2, start : start + HALF] = (
-                jnp.concatenate([block] * (HALF // PERIOD), axis=0) * mask
-            )
-            before = after
-
-
-def coarse_table(kernel):
-    pairs = (kernel.shape[0] + 1) // 2
-    return pl.pallas_call(
-        coarse_table_kernel,
-        grid=(pairs,),
-        in_specs=[pl.BlockSpec(kernel.shape, lambda i: (0, 0, 0))],
-        out_specs=pl.BlockSpec((1, SHIFTS, 2 * LZ, LZ), lambda i: (i, 0, 0, 0)),
-        out_shape=jax.ShapeDtypeStruct((pairs, SHIFTS, 2 * LZ, LZ), jnp.bfloat16),
-        scratch_shapes=[pltpu.VMEM((SPAN_PAD, LZ), jnp.float32)],
-        name="coarse_table",
-        compiler_params=pltpu.CompilerParams(vmem_limit_bytes=VMEM_BYTES),
-    )(kernel)
 
 
 def three_terms(value):
@@ -284,11 +320,24 @@
     )(*pieces)
 
 
-def fine_kernel(fine_ref, tap_ref, out_ref, pair_ref, row_ref, even_ref, odd_ref):
+def fine_kernel(
+    fine_ref,
+    tap_ref,
+    coarse_tap_ref,
+    out_ref,
+    coarse_ref,
+    pair_ref,
+    row_ref,
+    coarse_row_ref,
+    even_ref,
+    odd_ref,
+):
     side = tap_ref.shape[0]
     row_ref[...] = jnp.zeros_like(row_ref)
+    coarse_row_ref[...] = jnp.zeros_like(coarse_row_ref)
     for plane in range(side):
         row_ref[plane, 1 : 1 + side] = tap_rows(tap_ref[plane])
+        coarse_row_ref[plane, 1 : 1 + side] = tap_rows(coarse_tap_ref[plane])
     for shift in range(SHIFTS):
         halves = [fine_ref[:, pl.ds(2 * shift + part, 16, stride=2)] for part in range(2)]
         pair_ref[shift] = (
@@ -301,6 +350,20 @@
         for band in range(BANDS):
             block = turned(row_ref[plane, band : band + 1]).astype(jnp.bfloat16)
             table_ref[band] = jnp.concatenate([block] * (LZ // PERIOD), axis=0) * mask
+
+    def build_coarse(index, part):
+        plane = 2 * index + part
+        lower_half = lax.broadcasted_iota(jnp.int32, (PERIOD, LZ), 1) < HALF
+        mask = near_mask(HALF, HALF)
+        before = turned(coarse_row_ref[plane, 0:1])
+        for band in range(BANDS - 1):
+            after = turned(coarse_row_ref[plane, band + 1 : band + 2])
+            block = jnp.where(lower_half, after, before).astype(jnp.bfloat16)
+            start = part * LZ + (band % 2) * HALF
+            coarse_ref[index, band // 2, start : start + HALF] = (
+                jnp.concatenate([block] * (HALF // PERIOD), axis=0) * mask
+            )
+            before = after
 
     def multiply(table_ref, plane):
         rows = pl.ds(pl.multiple_of(plane * 16, 16), SPAN * 16)
@@ -321,28 +384,38 @@
     def two_planes(index, carry):
         plane = 2 * index
         build(odd_ref, plane + 1)
+        build_coarse(index, 0)
         multiply(even_ref, plane)
         build(even_ref, plane + 2)
+        build_coarse(index, 1)
         multiply(odd_ref, plane + 1)
         return carry
 
     lax.fori_loop(0, side // 2, two_planes, 0)
+    build_coarse(side // 2, 0)
+    build_coarse(side // 2, 1)
     multiply(even_ref, side - 1)
 
 
-def fine_sums(fine, kernel):
+def fine_sums(fine, kernel, kernel_coarse):
+    side = kernel.shape[0]
+    pairs = (side + 1) // 2
     return pl.pallas_call(
         fine_kernel,
-        out_shape=jax.ShapeDtypeStruct((SPAN * 16, 2 * LZ), jnp.float32),
+        out_shape=(
+            jax.ShapeDtypeStruct((SPAN * 16, 2 * LZ), jnp.float32),
+            jax.ShapeDtypeStruct((pairs, SHIFTS, 2 * LZ, LZ), jnp.bfloat16),
+        ),
         scratch_shapes=[
             pltpu.VMEM((SHIFTS, PLANES * 16, 2 * LZ), jnp.bfloat16),
-            pltpu.VMEM((kernel.shape[0], SPAN_PAD, LZ), jnp.float32),
+            pltpu.VMEM((side, SPAN_PAD, LZ), jnp.float32),
+            pltpu.VMEM((2 * pairs, SPAN_PAD, LZ), jnp.float32),
             pltpu.VMEM((BANDS, LZ, LZ), jnp.bfloat16),
             pltpu.VMEM((BANDS, LZ, LZ), jnp.bfloat16),
         ],
         name="fine",
         compiler_params=pltpu.CompilerParams(vmem_limit_bytes=VMEM_BYTES),
-    )(fine, kernel)
+    )(fine, kernel, kernel_coarse)
 
 
 def coarse_kernel(
@@ -433,10 +506,16 @@
         even = (before + 6.0 * middle + after) * 0.125
         odd = (middle + after) * 0.5
         sums = sums_ref[...].reshape(SPAN, 16, 2 * LZ)
-        join_ref[:, pl.ds(0, 16, stride=2)] = sums[:, :, :LZ] + even
-        join_ref[:, pl.ds(1, 16, stride=2)] = sums[:, :, LZ:] + odd
-        grid_ref[...] = join_ref[:LX, :LY]
-        face = join_ref[:, :SPAN_PAD].reshape(SPAN * SPAN_PAD, LZ)
+        join_ref[...] = jnp.zeros_like(join_ref)
+        for plane in range(SPAN):
+            start = plane * 32
+            join_ref[pl.ds(start, 16, stride=2)] = sums[plane, :, :LZ] + even[plane]
+            join_ref[pl.ds(start + 1, 16, stride=2)] = sums[plane, :, LZ:] + odd[plane]
+        for plane in range(LX):
+            grid_ref[plane] = join_ref[plane * 32 : plane * 32 + LY]
+        inside = [join_ref[plane * 32 : plane * 32 + LY] for plane in range(SPAN)]
+        outside = [join_ref[pl.ds(column, SPAN_PAD, stride=32)] for column in range(LY, SPAN)]
+        face = jnp.concatenate(inside + outside, axis=0)
         face_high = face.astype(jnp.bfloat16)
         face_low = (face - face_high.astype(jnp.float32)).astype(jnp.bfloat16)
         face_ref[:, :LZ] = face_high
@@ -463,11 +542,11 @@
         in_specs=specs,
         out_specs=(
             pl.BlockSpec((LX, LY, LZ), lambda i: (0, 0, 0)),
-            pl.BlockSpec((SPAN * SPAN_PAD, 2 * LZ), lambda i: (0, 0)),
+            pl.BlockSpec((FACE, 2 * LZ), lambda i: (0, 0)),
         ),
         out_shape=(
             jax.ShapeDtypeStruct((LX, LY, LZ), jnp.float32),
-            jax.ShapeDtypeStruct((SPAN * SPAN_PAD, 2 * LZ), jnp.bfloat16),
+            jax.ShapeDtypeStruct((FACE, 2 * LZ), jnp.bfloat16),
         ),
         scratch_shapes=[
             pltpu.VMEM((COARSE_IN + 1, 40, LZ), jnp.float32),
@@ -475,7 +554,7 @@
             pltpu.VMEM((COARSE_OUT * 8, LZ), jnp.float32),
             pltpu.VMEM((COARSE_OUT, 16, LZ), jnp.float32),
             pltpu.VMEM((SPAN, 24, LZ), jnp.float32),
-            pltpu.VMEM((SPAN, 32, LZ), jnp.float32),
+            pltpu.VMEM((SPAN_PAD * 32, LZ), jnp.float32),
         ],
         name="coarse",
         compiler_params=pltpu.CompilerParams(vmem_limit_bytes=VMEM_BYTES),
@@ -483,10 +562,13 @@
 
 
 def on_device(bead_charge, bead_cell, bead_count, interp_weights, kernel_fine, kernel_coarse):
-    own, up, down = spread_beads(bead_count, bead_charge, bead_cell, interp_weights)
+    beads = [
+        pltpu.with_memory_space_constraint(value, pltpu.HBM)
+        for value in (bead_charge, bead_cell, interp_weights)
+    ]
+    own, up, down, *tables = spread_beads(bead_count, *beads)
     below = from_behind(up, "gx", 1)
     above = from_behind(down, "gx", -1)
-    table_coarse = coarse_table(kernel_coarse)
     wraps = lax.axis_size("gy") == 2
     pieces = [own, below, above]
     for steps in (1,) if wraps else (1, -1):
@@ -494,7 +576,7 @@
     fine, coarse, coarse_up, coarse_down = gather_fine(pieces)
     coarse_below = from_behind(coarse_up, "gx", 1)
     coarse_above = from_behind(coarse_down, "gx", -1)
-    sums = fine_sums(fine, kernel_fine)
+    sums, table_coarse = fine_sums(fine, kernel_fine, kernel_coarse)
     low = high = None
     if not wraps:
         joined = jnp.concatenate([coarse_below, coarse, coarse_above], axis=0)
@@ -503,7 +585,7 @@
     potential_grid, face = potentials(
         coarse, coarse_below, coarse_above, low, high, table_coarse, sums
     )
-    bead_potential = read_beads(bead_count, face, bead_cell, interp_weights)
+    bead_potential = read_beads(bead_count, face, tables)
     return (bead_potential, potential_grid)
 
 

time: 63.7 us -> 52.2 us (0.82)
  Pallas kernels: 40.6 us -> 31 us
  local copies, waits for them, and re-layouts: 3.62 us -> 1.79 us
    pallas_call x4 -> x3, Pallas kernels: 36.2 us -> 26.6 us  [the longest x1 11.3 us: spread_beads(): pl.pallas_call(spread_kernel, grid=(slots // BLOCK,), in_specs=[pl.BlockS...]
    unnamed x14 -> x4, local copies, waits for them, and re-layouts: 3.62 us -> 1.79 us
  transfers between devices with their start and end apart: 7 -> 7, of which waited for: 3 -> 3; matrix products, arithmetic and copies ran while one was open for 0% -> 0% of each run, Pallas kernels for 19% -> 18%
where the time goes in v1:
time: 52.2 us; the launch traced here: 52 us
  Pallas kernels  31 us (59%)
  starting transfers between devices  13.3 us (25%)
  waiting for transfers between devices  4.66 us (9%)
  local copies, waits for them, and re-layouts  1.79 us (3%)
  between operations  1.32 us (3%)
    ppermute x7, starting transfers between devices, from_behind(): return lax.ppermute(value, axis, pairs)  13.3 us
    pallas_call x1, Pallas kernels, spread_beads(): pl.pallas_call(spread_kernel, grid=(slots // BLOCK,), in_specs=[pl.BlockS...  11.3 us
    pallas_call x1, Pallas kernels, fine_sums(): pl.pallas_call(fine_kernel, out_shape=(jax.ShapeDtypeStruct((SPAN * 16, 2...  9.36 us
    pallas_call x1, Pallas kernels, read_beads(): pl.pallas_call(read_kernel, grid=(slots // BLOCK,), in_specs=[pl.BlockSpe...  5.97 us
    ppermute x7, waiting for transfers between devices, from_behind(): return lax.ppermute(value, axis, pairs)  4.66 us
    pallas_call x1, Pallas kernels, potentials(): pl.pallas_call(body, grid=(table.shape[0],), in_specs=specs, out_specs=(p...  3.86 us
    unnamed x4, local copies, waits for them, and re-layouts  1.79 us
  transfers between devices with their start and end apart: 7, of which 3 were waited for; matrix products, arithmetic and copies ran while one was open for 0% of the time, Pallas kernels for 18%

profile of v1, /device:TPU:0, one launch (start us, length us, event | category | flops | bytes accessed | tf_op | source)
XLA Modules:
  0.0 52.0 jit_solution(15050121156591607623)
XLA Ops:
  1.3 11.3 %spread.1 = (f32[456,128]{1,0:T(8,128)S(1)}, f32[11,24,128]{2,1,0:T(8,128)S(1)}, f32[11,24,128]{2,1,0:T(8,128)S(1)}, bf16[128,16384]{1,0:T(8,128)(2,1)S(1)}, f32...) custom-call(s32[1,1]{1,0:T(1,128)S(6)} %copy.8.count_ref, f32[1,1,16384]{2,1,0:T(1,128)} %charge_ref.1, ...), custom_call_target="tpu_custom_call" | custom-call | tf_op jit(solution)/shard_map/spread/pallas_call | solution.py:182
  12.6 3.0 %collective-permute-start = (f32[11,24,128]{2,1,0:T(8,128)S(1)}, f32[11,24,128]{2,1,0:T(8,128)S(1)}, u32[]{:S(2)}, u32[]{:S(2)}) collective-permute-start(f32[11,24,128]{2,1,0:T(8,128)S(1)} %get-tuple-element.17), channel_id=1, source_target_pairs={{0,2},{2,4},{4,6},{6,8},{8,10},{10,12},{12,14},{14,16},{16,18},{18... | collective-permute-start | bytes 405512 | tf_op jit(solution)/shard_map/ppermute | solution.py:35
  15.6 4.1 %collective-permute-start.1 = (f32[11,24,128]{2,1,0:T(8,128)S(1)}, f32[11,24,128]{2,1,0:T(8,128)S(1)}, u32[]{:S(2)}, u32[]{:S(2)}) collective-permute-start(f32[11,24,128]{2,1,0:T(8,128)S(1)} %get-tuple-element.18), channel_id=1, source_target_pairs={{0,30},{2,0},{4,2},{6,4},{8,6},{10,8},{12,10},{14,12},{16,14},{18,... | collective-permute-start | bytes 405512 | tf_op jit(solution)/shard_map/ppermute | solution.py:35
  19.7 0.0 collective-permute-start.2
  19.7 3.6 %collective-permute-done.refs_1_ = f32[11,24,128]{2,1,0:T(8,128)S(1)} collective-permute-done((f32[11,24,128]{2,1,0:T(8,128)S(1)}, f32[11,24,128]{2,1,0:T(8,128)S(1)}, u32[]{:S(2)}, u32[]{:S(2)}) %collective-permute-start) | collective-permute-done | bytes 135200 | tf_op jit(solution)/shard_map/ppermute | solution.py:35
  23.3 0.0 collective-permute-start.3
  23.3 0.0 collective-permute-done.1.refs_2_
  23.3 0.5 collective-permute-start.4
  23.8 0.0 collective-permute-done.2.refs_3_
  23.8 0.8 %collective-permute-done.3.refs_4_ = f32[11,24,128]{2,1,0:T(8,128)S(1)} collective-permute-done((f32[11,24,128]{2,1,0:T(8,128)S(1)}, f32[11,24,128]{2,1,0:T(8,128)S(1)}, u32[]{:S(2)}, u32[]{:S(2)}) %collective-permute-start.3) | collective-permute-done | bytes 135200 | tf_op jit(solution)/shard_map/ppermute | solution.py:35
  24.7 0.2 collective-permute-done.4.refs_5_
  24.8 0.5 gather.1
  25.3 1.4 %collective-permute-start.5 = (bf16[6,16,128]{2,1,0:T(8,128)(2,1)S(1)}, bf16[6,16,128]{2,1,0:T(8,128)(2,1)S(1)}, u32[]{:S(2)}, u32[]{:S(2)}) collective-permute-start(bf16[6,16,128]{2,1,0:T(8,128)(2,1)S(1)} %get-tuple-element.20), channel_id=1, source_target_pairs={{0,2},{2,4},{4,6},{6,8},{8,10},{10,12},{12,14},{14,16},{16,18},{18... | collective-permute-start | bytes 73736 | tf_op jit(solution)/shard_map/ppermute | solution.py:35
  26.7 4.3 %collective-permute-start.6 = (bf16[6,16,128]{2,1,0:T(8,128)(2,1)S(1)}, bf16[6,16,128]{2,1,0:T(8,128)(2,1)S(1)}, u32[]{:S(2)}, u32[]{:S(2)}) collective-permute-start(bf16[6,16,128]{2,1,0:T(8,128)(2,1)S(1)} %get-tuple-element.21), channel_id=1, source_target_pairs={{0,30},{2,0},{4,2},{6,4},{8,6},{10,8},{12,10},{14,12},{16,14},{18,... | collective-permute-start | bytes 73736 | tf_op jit(solution)/shard_map/ppermute | solution.py:35
  31.0 0.0 copy-start
  31.0 0.9 %copy-done = bf16[17,17,17]{2,1,0:T(8,128)(2,1)S(1)} copy-done((bf16[17,17,17]{2,1,0:T(8,128)(2,1)S(1)}, bf16[17,17,17]{2,1,0:T(8,128)(2,1)}, u32[]{:S(2)}) %copy-start) | copy-done | bytes 9850
  31.9 0.0 copy-start.1
  31.9 0.9 %copy-done.1 = bf16[17,17,17]{2,1,0:T(8,128)(2,1)S(1)} copy-done((bf16[17,17,17]{2,1,0:T(8,128)(2,1)S(1)}, bf16[17,17,17]{2,1,0:T(8,128)(2,1)}, u32[]{:S(2)}) %copy-start.1) | copy-done | bytes 9850
  32.8 9.4 %fine.1 = (f32[304,256]{1,0:T(8,128)S(1)}, bf16[9,9,256,128]{3,2,1,0:T(8,128)(2,1)S(1)}) custom-call(f32[35,48,128]{2,1,0:T(8,128)S(1)} %get-tuple-element.22.fine_ref, bf16[17,17,17]{2,1,0:T(8,128)(2,1)S(1)} %copy-done, bf16[17,17,17]{2,1,0:T(8,128)(2,1)S(1)} %copy-done.1), custom_call_target="tpu_custom_call" | custom-call | tf_op jit(solution)/shard_map/fine/pallas_call | solution.py:403
  42.1 0.0 collective-permute-done.5.refs_1_
  42.2 0.0 collective-permute-done.6.refs_2_
  42.2 3.9 %coarse.1 = (f32[16,16,128]{2,1,0:T(8,128)}, bf16[376,256]{1,0:T(8,128)(2,1)S(1)}) custom-call(bf16[16,16,128]{2,1,0:T(8,128)(2,1)S(1)} %get-tuple-element.19.refs_0_, bf16[6,16,128]{2,1,0:T(8,128)(2,1)S(1)} %collective-permute-done.5.refs_1_, bf16[6,16,128]{2,1,0:T(8,128)(2,1)S(1)} %collective-permute-done.6.refs_2_, ...), custom_call_target="tpu_custom_call" | custom-call | tf_op jit(solution)/shard_map/coarse/pallas_call | solution.py:539
  46.0 6.0 %read.1 = f32[1,1,16384]{2,1,0:T(1,128)} custom-call(s32[1,1]{1,0:T(1,128)S(6)} %copy.8.count_ref, bf16[376,256]{1,0:T(8,128)(2,1)S(1)} %get-tuple-element.25.grid_ref, bf16[128,16384]{1,0:T(8,128)(2,1)S(1)} %get-tuple-element.26.depth_ref, f32[24,16384]{1,0:T(8,128)S(1)} %get-tuple-element.27.first_ref, f32[24,16384]{1,0:T(8,128)S(1)} %get-tuple-element.28.second_ref), custom_call_target="tpu_custom_call" | custom-call | tf_op jit(solution)/shard_map/read/pallas_call | solution.py:199
Async XLA Ops:
  12.6 10.7 %collective-permute-start = (f32[11,24,128]{2,1,0:T(8,128)S(1)}, f32[11,24,128]{2,1,0:T(8,128)S(1)}, u32[]{:S(2)}, u32[]{:S(2)}) collective-permute-start(f32[11,24,128]{2,1,0:T(8,128)S(1)} %get-tuple-element.17), channel_id=1, source_target_pairs={{0,2},{2,4},{4,6},{6,8},{8,10},{10,12},{12,14},{14,16},{16,18},{18... | collective-permute-start | bytes 405512 | tf_op jit(solution)/shard_map/ppermute | solution.py:35
  15.6 7.7 %collective-permute-start.1 = (f32[11,24,128]{2,1,0:T(8,128)S(1)}, f32[11,24,128]{2,1,0:T(8,128)S(1)}, u32[]{:S(2)}, u32[]{:S(2)}) collective-permute-start(f32[11,24,128]{2,1,0:T(8,128)S(1)} %get-tuple-element.18), channel_id=1, source_target_pairs={{0,30},{2,0},{4,2},{6,4},{8,6},{10,8},{12,10},{14,12},{16,14},{18,... | collective-permute-start | bytes 405512 | tf_op jit(solution)/shard_map/ppermute | solution.py:35
  19.7 4.1 %collective-permute-start.2 = (f32[456,128]{1,0:T(8,128)S(1)}, f32[456,128]{1,0:T(8,128)S(1)}, u32[]{:S(2)}, u32[]{:S(2)}) collective-permute-start(f32[456,128]{1,0:T(8,128)S(1)} %get-tuple-element.16.refs_0_), channel_id=1, source_target_pairs={{0,1},{1,0},{2,3},{3,2},{4,5},{5,4},{6,7},{7,6},{8,9},{9,8},{10,11... | collective-permute-start | bytes 700424 | tf_op jit(solution)/shard_map/ppermute | solution.py:35
  23.3 1.4 %collective-permute-start.3 = (f32[11,24,128]{2,1,0:T(8,128)S(1)}, f32[11,24,128]{2,1,0:T(8,128)S(1)}, u32[]{:S(2)}, u32[]{:S(2)}) collective-permute-start(f32[11,24,128]{2,1,0:T(8,128)S(1)} %collective-permute-done.refs_1_), channel_id=1, source_target_pairs={{0,1},{1,0},{2,3},{3,2},{4,5},{5,4},{6,7},{7,6},{8,9},{9,8},{10,11... | collective-permute-start | bytes 405512 | tf_op jit(solution)/shard_map/ppermute | solution.py:35
  23.3 1.5 %collective-permute-start.4 = (f32[11,24,128]{2,1,0:T(8,128)S(1)}, f32[11,24,128]{2,1,0:T(8,128)S(1)}, u32[]{:S(2)}, u32[]{:S(2)}) collective-permute-start(f32[11,24,128]{2,1,0:T(8,128)S(1)} %collective-permute-done.1.refs_2_), channel_id=1, source_target_pairs={{0,1},{1,0},{2,3},{3,2},{4,5},{5,4},{6,7},{7,6},{8,9},{9,8},{10,11... | collective-permute-start | bytes 405512 | tf_op jit(solution)/shard_map/ppermute | solution.py:35
  25.3 16.8 %collective-permute-start.5 = (bf16[6,16,128]{2,1,0:T(8,128)(2,1)S(1)}, bf16[6,16,128]{2,1,0:T(8,128)(2,1)S(1)}, u32[]{:S(2)}, u32[]{:S(2)}) collective-permute-start(bf16[6,16,128]{2,1,0:T(8,128)(2,1)S(1)} %get-tuple-element.20), channel_id=1, source_target_pairs={{0,2},{2,4},{4,6},{6,8},{8,10},{10,12},{12,14},{14,16},{16,18},{18... | collective-permute-start | bytes 73736 | tf_op jit(solution)/shard_map/ppermute | solution.py:35
  26.7 15.5 %collective-permute-start.6 = (bf16[6,16,128]{2,1,0:T(8,128)(2,1)S(1)}, bf16[6,16,128]{2,1,0:T(8,128)(2,1)S(1)}, u32[]{:S(2)}, u32[]{:S(2)}) collective-permute-start(bf16[6,16,128]{2,1,0:T(8,128)(2,1)S(1)} %get-tuple-element.21), channel_id=1, source_target_pairs={{0,30},{2,0},{4,2},{6,4},{8,6},{10,8},{12,10},{14,12},{16,14},{18,... | collective-permute-start | bytes 73736 | tf_op jit(solution)/shard_map/ppermute | solution.py:35
  31.0 0.9 %copy-start = (bf16[17,17,17]{2,1,0:T(8,128)(2,1)S(1)}, bf16[17,17,17]{2,1,0:T(8,128)(2,1)}, u32[]{:S(2)}) copy-start(bf16[17,17,17]{2,1,0:T(8,128)(2,1)} %tap_ref.1) | copy-start | bytes 29482
  31.9 0.9 %copy-start.1 = (bf16[17,17,17]{2,1,0:T(8,128)(2,1)S(1)}, bf16[17,17,17]{2,1,0:T(8,128)(2,1)}, u32[]{:S(2)}) copy-start(bf16[17,17,17]{2,1,0:T(8,128)(2,1)} %coarse_tap_ref.1) | copy-start | bytes 29482

commit v2 on v1

--- a/solution.py
+++ b/solution.py
@@ -19,7 +19,10 @@
 VMEM_BYTES = 24 * 1024 * 1024
 REACH = 11
 PLANES = SPAN + 2 * RADIUS
+PLANES_PAD = 40
 COLUMNS = 48
+NEAR = (SPAN + 1) * 8
+FAR = 2 * SPAN_PAD
 SHIFTS = RADIUS + 1
 BANDS = 2 * RADIUS + 3
 HALF = LZ // 2
@@ -76,12 +79,16 @@
     charge_ref,
     cell_ref,
     weight_ref,
+    tap_ref,
+    coarse_tap_ref,
     out_ref,
     up_ref,
     down_ref,
     depth_ref,
     first_ref,
     second_ref,
+    row_ref,
+    coarse_row_ref,
     total_ref,
     order_ref,
 ):
@@ -90,6 +97,12 @@
     @pl.when(step == 0)
     def _():
         total_ref[...] = jnp.zeros_like(total_ref)
+        row_ref[...] = jnp.zeros_like(row_ref)
+        coarse_row_ref[...] = jnp.zeros_like(coarse_row_ref)
+        side = tap_ref.shape[0]
+        for plane in range(side):
+            row_ref[plane, 1 : 1 + side] = tap_rows(tap_ref[plane])
+            coarse_row_ref[plane, 1 : 1 + side] = tap_rows(coarse_tap_ref[plane])
 
     dims = (((1,), (1,)), ((), ()))
     total = None
@@ -99,9 +112,10 @@
         weights = weight_ref[0, 0, :, beads].astype(jnp.float32)
         first, second, depth = bead_tables(cells, weights)
         depth = depth.astype(jnp.bfloat16)
-        depth_ref[:, beads] = depth
-        first_ref[:, beads] = first
-        second_ref[:, beads] = second
+        kept = pl.ds(pl.multiple_of(step * BLOCK, BLOCK) + start, CHUNK)
+        depth_ref[:, kept] = depth
+        first_ref[:, kept] = first
+        second_ref[:, kept] = second
         slots = lax.broadcasted_iota(jnp.int32, cells.shape, 1) + (step * BLOCK + start)
         amount = jnp.where(slots < count_ref[0, 0], charge_ref[0, :, beads], 0.0)
         face = face_rows(first * amount, second)
@@ -133,14 +147,15 @@
     step = pl.program_id(0)
     for start in range(0, BLOCK, READ_CHUNK):
         beads = slice(start, start + READ_CHUNK)
-        depth = depth_ref[:, beads]
+        kept = pl.ds(pl.multiple_of(step * BLOCK, BLOCK) + start, READ_CHUNK)
+        depth = depth_ref[:, kept]
         along = jnp.dot(
             grid_ref[...],
             jnp.concatenate([depth, depth], axis=0),
             preferred_element_type=jnp.float32,
         )
-        first = first_ref[:, beads]
-        second = second_ref[:, beads]
+        first = first_ref[:, kept]
+        second = second_ref[:, kept]
         inside = first[0:1] * along[0:LY]
         for row in range(1, SPAN):
             inside = inside + first[row : row + 1] * along[row * LY : (row + 1) * LY]
@@ -163,14 +178,15 @@
 
 
 def table_specs():
-    return [pl.BlockSpec((rows, BLOCK), lambda i: (0, i)) for rows in (LZ, SPAN_PAD, SPAN_PAD)]
-
-
-def spread_beads(count, charge, cell, weights):
+    return [pl.BlockSpec(memory_space=pltpu.VMEM)] * 3
+
+
+def spread_beads(count, charge, cell, weights, kernel, kernel_coarse):
     slots = charge.shape[2]
     row = pl.BlockSpec((1, 1, BLOCK), lambda i: (0, 0, i))
     weight = pl.BlockSpec((1, 1, 12, BLOCK), lambda i: (0, 0, 0, i))
     edge = (REACH, SPAN_PAD, LZ)
+    side = kernel.shape[0]
     shapes = [
         jax.ShapeDtypeStruct((SPAN * SPAN_PAD, LZ), jnp.float32),
         jax.ShapeDtypeStruct(edge, jnp.float32),
@@ -178,12 +194,17 @@
         jax.ShapeDtypeStruct((LZ, slots), jnp.bfloat16),
         jax.ShapeDtypeStruct((SPAN_PAD, slots), jnp.float32),
         jax.ShapeDtypeStruct((SPAN_PAD, slots), jnp.float32),
+        jax.ShapeDtypeStruct((side, SPAN_PAD, LZ), jnp.float32),
+        jax.ShapeDtypeStruct((side + 1, SPAN_PAD, LZ), jnp.float32),
     ]
+    tap_specs = [whole_spec(kernel.shape)] * 2
     return pl.pallas_call(
         spread_kernel,
         grid=(slots // BLOCK,),
-        in_specs=[pl.BlockSpec(memory_space=pltpu.SMEM), row, row, weight],
-        out_specs=[whole_spec(part.shape) for part in shapes[:3]] + table_specs(),
+        in_specs=[pl.BlockSpec(memory_space=pltpu.SMEM), row, row, weight] + tap_specs,
+        out_specs=[whole_spec(part.shape) for part in shapes[:3]]
+        + table_specs()
+        + [whole_spec(part.shape) for part in shapes[6:]],
         out_shape=shapes,
         scratch_shapes=[
             pltpu.VMEM((FACE, LZ), jnp.float32),
@@ -191,7 +212,7 @@
         ],
         name="spread",
         compiler_params=pltpu.CompilerParams(vmem_limit_bytes=VMEM_BYTES),
-    )(count, charge, cell, weights)
+    )(count, charge, cell, weights, kernel, kernel_coarse)
 
 
 def read_beads(count, grid, tables):
@@ -283,6 +304,7 @@
             axis=0,
         )
         fine_ref[plane] = value.astype(jnp.bfloat16).astype(jnp.float32)
+    fine_ref[PLANES:] = jnp.zeros_like(fine_ref[PLANES:])
     spline = (0.125, 0.5, 0.75, 0.5, 0.125)
     for plane in range(KNOWN):
         total = spline[0] * fine_ref[2 * plane]
@@ -309,7 +331,7 @@
     return pl.pallas_call(
         gather_kernel,
         out_shape=(
-            jax.ShapeDtypeStruct((PLANES, COLUMNS, LZ), jnp.float32),
+            jax.ShapeDtypeStruct((PLANES_PAD, COLUMNS, LZ), jnp.float32),
             jax.ShapeDtypeStruct((KNOWN, KNOWN, LZ), jnp.bfloat16),
             edge,
             edge,
@@ -322,27 +344,24 @@
 
 def fine_kernel(
     fine_ref,
-    tap_ref,
-    coarse_tap_ref,
+    row_ref,
+    coarse_row_ref,
     out_ref,
     coarse_ref,
     pair_ref,
-    row_ref,
-    coarse_row_ref,
     even_ref,
     odd_ref,
 ):
-    side = tap_ref.shape[0]
-    row_ref[...] = jnp.zeros_like(row_ref)
-    coarse_row_ref[...] = jnp.zeros_like(coarse_row_ref)
-    for plane in range(side):
-        row_ref[plane, 1 : 1 + side] = tap_rows(tap_ref[plane])
-        coarse_row_ref[plane, 1 : 1 + side] = tap_rows(coarse_tap_ref[plane])
+    side = row_ref.shape[0]
+    flat_ref = fine_ref.reshape(PLANES_PAD * COLUMNS, LZ)
+    kept = pair_ref.shape[2] // 8
     for shift in range(SHIFTS):
-        halves = [fine_ref[:, pl.ds(2 * shift + part, 16, stride=2)] for part in range(2)]
-        pair_ref[shift] = (
-            jnp.concatenate(halves, axis=2).reshape(PLANES * 16, 2 * LZ).astype(jnp.bfloat16)
-        )
+        halves = [fine_ref[:, pl.ds(2 * shift + part, 8, stride=2)] for part in range(2)]
+        both = jnp.concatenate(halves, axis=2)
+        for part in range(2):
+            pair_ref[part, shift] = (
+                both[part : part + kept].reshape(kept * 8, 2 * LZ).astype(jnp.bfloat16)
+            )
     out_ref[...] = jnp.zeros_like(out_ref)
 
     def build(table_ref, plane):
@@ -365,15 +384,23 @@
             )
             before = after
 
-    def multiply(table_ref, plane):
-        rows = pl.ds(pl.multiple_of(plane * 16, 16), SPAN * 16)
+    def multiply(table_ref, plane, part):
+        rows = pl.ds(pl.multiple_of((plane - part) * 8, 16), NEAR)
+        far = []
+        for pair in range(SHIFTS + 1):
+            column = plane * COLUMNS + LY + 2 * pair
+            halves = [
+                flat_ref[pl.ds(column + half, SPAN_PAD, stride=COLUMNS)] for half in range(2)
+            ]
+            far.append(jnp.concatenate(halves, axis=1))
         total = out_ref[...]
         for shift in range(SHIFTS):
             band = 2 * shift + 1
             upper = jnp.concatenate([table_ref[band], table_ref[band - 1]], axis=1)
             lower = jnp.concatenate([table_ref[band + 1], table_ref[band]], axis=1)
+            outer = jnp.concatenate(far[shift : shift + 2], axis=0).astype(jnp.bfloat16)
             total = total + jnp.dot(
-                pair_ref[shift, rows],
+                jnp.concatenate([pair_ref[part, shift, rows], outer], axis=0),
                 jnp.concatenate([upper, lower], axis=0),
                 preferred_element_type=jnp.float32,
             )
@@ -385,37 +412,35 @@
         plane = 2 * index
         build(odd_ref, plane + 1)
         build_coarse(index, 0)
-        multiply(even_ref, plane)
+        multiply(even_ref, plane, 0)
         build(even_ref, plane + 2)
         build_coarse(index, 1)
-        multiply(odd_ref, plane + 1)
+        multiply(odd_ref, plane + 1, 1)
         return carry
 
     lax.fori_loop(0, side // 2, two_planes, 0)
     build_coarse(side // 2, 0)
     build_coarse(side // 2, 1)
-    multiply(even_ref, side - 1)
-
-
-def fine_sums(fine, kernel, kernel_coarse):
-    side = kernel.shape[0]
+    multiply(even_ref, side - 1, 0)
+
+
+def fine_sums(fine, rows, rows_coarse):
+    side = rows.shape[0]
     pairs = (side + 1) // 2
     return pl.pallas_call(
         fine_kernel,
         out_shape=(
-            jax.ShapeDtypeStruct((SPAN * 16, 2 * LZ), jnp.float32),
+            jax.ShapeDtypeStruct((NEAR + FAR, 2 * LZ), jnp.float32),
             jax.ShapeDtypeStruct((pairs, SHIFTS, 2 * LZ, LZ), jnp.bfloat16),
         ),
         scratch_shapes=[
-            pltpu.VMEM((SHIFTS, PLANES * 16, 2 * LZ), jnp.bfloat16),
-            pltpu.VMEM((side, SPAN_PAD, LZ), jnp.float32),
-            pltpu.VMEM((2 * pairs, SPAN_PAD, LZ), jnp.float32),
+            pltpu.VMEM((2, SHIFTS, NEAR + 16 * RADIUS, 2 * LZ), jnp.bfloat16),
             pltpu.VMEM((BANDS, LZ, LZ), jnp.bfloat16),
             pltpu.VMEM((BANDS, LZ, LZ), jnp.bfloat16),
         ],
         name="fine",
         compiler_params=pltpu.CompilerParams(vmem_limit_bytes=VMEM_BYTES),
-    )(fine, kernel, kernel_coarse)
+    )(fine, rows, rows_coarse)
 
 
 def coarse_kernel(
@@ -505,12 +530,21 @@
         after = wide_ref[:, 2:18]
         even = (before + 6.0 * middle + after) * 0.125
         odd = (middle + after) * 0.5
-        sums = sums_ref[...].reshape(SPAN, 16, 2 * LZ)
+        near = sums_ref[:NEAR].reshape(SPAN + 1, 8, 2 * LZ)
         join_ref[...] = jnp.zeros_like(join_ref)
         for plane in range(SPAN):
             start = plane * 32
-            join_ref[pl.ds(start, 16, stride=2)] = sums[plane, :, :LZ] + even[plane]
-            join_ref[pl.ds(start + 1, 16, stride=2)] = sums[plane, :, LZ:] + odd[plane]
+            for part, refined in ((0, even[plane]), (1, odd[plane])):
+                join_ref[pl.ds(start + part, 8, stride=2)] = (
+                    near[plane, :, part * LZ : (part + 1) * LZ] + refined[:8]
+                )
+                join_ref[pl.ds(start + 16 + part, 8, stride=2)] = refined[8:]
+        for column in range(LY, SPAN):
+            pair, part = divmod(column - LY, 2)
+            rows = slice(NEAR + pair * SPAN_PAD, NEAR + (pair + 1) * SPAN_PAD)
+            join_ref[pl.ds(column, SPAN_PAD, stride=32)] += sums_ref[
+                rows, part * LZ : (part + 1) * LZ
+            ]
         for plane in range(LX):
             grid_ref[plane] = join_ref[plane * 32 : plane * 32 + LY]
         inside = [join_ref[plane * 32 : plane * 32 + LY] for plane in range(SPAN)]
@@ -564,9 +598,9 @@
 def on_device(bead_charge, bead_cell, bead_count, interp_weights, kernel_fine, kernel_coarse):
     beads = [
         pltpu.with_memory_space_constraint(value, pltpu.HBM)
-        for value in (bead_charge, bead_cell, interp_weights)
+        for value in (bead_charge, bead_cell, interp_weights, kernel_fine, kernel_coarse)
     ]
-    own, up, down, *tables = spread_beads(bead_count, *beads)
+    own, up, down, *tables, rows, rows_coarse = spread_beads(bead_count, *beads)
     below = from_behind(up, "gx", 1)
     above = from_behind(down, "gx", -1)
     wraps = lax.axis_size("gy") == 2
@@ -576,7 +610,7 @@
     fine, coarse, coarse_up, coarse_down = gather_fine(pieces)
     coarse_below = from_behind(coarse_up, "gx", 1)
     coarse_above = from_behind(coarse_down, "gx", -1)
-    sums, table_coarse = fine_sums(fine, kernel_fine, kernel_coarse)
+    sums, table_coarse = fine_sums(fine, rows, rows_coarse)
     low = high = None
     if not wraps:
         joined = jnp.concatenate([coarse_below, coarse, coarse_above], axis=0)

time: 52.2 us -> 47.8 us (0.916)
  Pallas kernels: 31 us -> 28.4 us
  local copies, waits for them, and re-layouts: 1.79 us -> 0 us
    pallas_call x2, Pallas kernels: 9.83 us -> 7.62 us  [the longest x1 7.15 us: fine_sums(): pl.pallas_call(fine_kernel, out_shape=(jax.ShapeDtypeStruct((NEAR + FAR,...]
    unnamed x4 -> x0, local copies, waits for them, and re-layouts: 1.79 us -> none
  transfers between devices with their start and end apart: 7 -> 7, of which waited for: 3 -> 3; matrix products, arithmetic and copies ran while one was open for 0% -> 0% of each run, Pallas kernels for 18% -> 15%
where the time goes in v2:
time: 47.8 us; the launch traced here: 47.6 us
  Pallas kernels  28.4 us (59%)
  starting transfers between devices  13.3 us (28%)
  waiting for transfers between devices  4.66 us (10%)
  between operations  1.32 us (3%)
    ppermute x7, starting transfers between devices, from_behind(): return lax.ppermute(value, axis, pairs)  13.3 us
    pallas_call x1, Pallas kernels, spread_beads(): pl.pallas_call(spread_kernel, grid=(slots // BLOCK,), in_specs=[pl.BlockS...  11.4 us
    pallas_call x1, Pallas kernels, fine_sums(): pl.pallas_call(fine_kernel, out_shape=(jax.ShapeDtypeStruct((NEAR + FAR,...  7.15 us
    pallas_call x1, Pallas kernels, read_beads(): pl.pallas_call(read_kernel, grid=(slots // BLOCK,), in_specs=[pl.BlockSpe...  5.48 us
    ppermute x7, waiting for transfers between devices, from_behind(): return lax.ppermute(value, axis, pairs)  4.66 us
    pallas_call x1, Pallas kernels, potentials(): pl.pallas_call(body, grid=(table.shape[0],), in_specs=specs, out_specs=(p...  3.9 us
  transfers between devices with their start and end apart: 7, of which 3 were waited for; matrix products, arithmetic and copies ran while one was open for 0% of the time, Pallas kernels for 15%

profile of v2, /device:TPU:0, one launch (start us, length us, event | category | flops | bytes accessed | tf_op | source)
XLA Modules:
  0.0 47.6 jit_solution(14281898256833210000)
XLA Ops:
  1.3 11.4 %spread.1 = (f32[456,128]{1,0:T(8,128)S(1)}, f32[11,24,128]{2,1,0:T(8,128)S(1)}, f32[11,24,128]{2,1,0:T(8,128)S(1)}, bf16[128,16384]{1,0:T(8,128)(2,1)S(1)}, f32...) custom-call(s32[1,1]{1,0:T(1,128)S(6)} %copy.8.count_ref, ...), custom_call_target="tpu_custom_call" | custom-call | tf_op jit(solution)/shard_map/spread/pallas_call | solution.py:201
  12.7 3.0 %collective-permute-start = (f32[11,24,128]{2,1,0:T(8,128)S(1)}, f32[11,24,128]{2,1,0:T(8,128)S(1)}, u32[]{:S(2)}, u32[]{:S(2)}) collective-permute-start(f32[11,24,128]{2,1,0:T(8,128)S(1)} %get-tuple-element.19), channel_id=1, source_target_pairs={{0,2},{2,4},{4,6},{6,8},{8,10},{10,12},{12,14},{14,16},{16,18},{18... | collective-permute-start | bytes 405512 | tf_op jit(solution)/shard_map/ppermute | solution.py:38
  15.7 4.0 %collective-permute-start.1 = (f32[11,24,128]{2,1,0:T(8,128)S(1)}, f32[11,24,128]{2,1,0:T(8,128)S(1)}, u32[]{:S(2)}, u32[]{:S(2)}) collective-permute-start(f32[11,24,128]{2,1,0:T(8,128)S(1)} %get-tuple-element.20), channel_id=1, source_target_pairs={{0,30},{2,0},{4,2},{6,4},{8,6},{10,8},{12,10},{14,12},{16,14},{18,... | collective-permute-start | bytes 405512 | tf_op jit(solution)/shard_map/ppermute | solution.py:38
  19.7 0.0 collective-permute-start.2
  19.8 3.6 %collective-permute-done.refs_1_ = f32[11,24,128]{2,1,0:T(8,128)S(1)} collective-permute-done((f32[11,24,128]{2,1,0:T(8,128)S(1)}, f32[11,24,128]{2,1,0:T(8,128)S(1)}, u32[]{:S(2)}, u32[]{:S(2)}) %collective-permute-start) | collective-permute-done | bytes 135200 | tf_op jit(solution)/shard_map/ppermute | solution.py:38
  23.4 0.0 collective-permute-start.3
  23.4 0.0 collective-permute-done.1.refs_2_
  23.4 0.5 %collective-permute-start.4 = (f32[11,24,128]{2,1,0:T(8,128)S(1)}, f32[11,24,128]{2,1,0:T(8,128)S(1)}, u32[]{:S(2)}, u32[]{:S(2)}) collective-permute-start(f32[11,24,128]{2,1,0:T(8,128)S(1)} %collective-permute-done.1.refs_2_), channel_id=1, source_target_pairs={{0,1},{1,0},{2,3},{3,2},{4,5},{5,4},{6,7},{7,6},{8,9},{9,8},{10,11... | collective-permute-start | bytes 405512 | tf_op jit(solution)/shard_map/ppermute | solution.py:38
  23.9 0.0 collective-permute-done.2.refs_3_
  23.9 0.8 %collective-permute-done.3.refs_4_ = f32[11,24,128]{2,1,0:T(8,128)S(1)} collective-permute-done((f32[11,24,128]{2,1,0:T(8,128)S(1)}, f32[11,24,128]{2,1,0:T(8,128)S(1)}, u32[]{:S(2)}, u32[]{:S(2)}) %collective-permute-start.3) | collective-permute-done | bytes 135200 | tf_op jit(solution)/shard_map/ppermute | solution.py:38
  24.7 0.2 collective-permute-done.4.refs_5_
  24.9 0.5 gather.1
  25.4 1.4 %collective-permute-start.5 = (bf16[6,16,128]{2,1,0:T(8,128)(2,1)S(1)}, bf16[6,16,128]{2,1,0:T(8,128)(2,1)S(1)}, u32[]{:S(2)}, u32[]{:S(2)}) collective-permute-start(bf16[6,16,128]{2,1,0:T(8,128)(2,1)S(1)} %get-tuple-element.22), channel_id=1, source_target_pairs={{0,2},{2,4},{4,6},{6,8},{8,10},{10,12},{12,14},{14,16},{16,18},{18... | collective-permute-start | bytes 73736 | tf_op jit(solution)/shard_map/ppermute | solution.py:38
  26.8 4.3 %collective-permute-start.6 = (bf16[6,16,128]{2,1,0:T(8,128)(2,1)S(1)}, bf16[6,16,128]{2,1,0:T(8,128)(2,1)S(1)}, u32[]{:S(2)}, u32[]{:S(2)}) collective-permute-start(bf16[6,16,128]{2,1,0:T(8,128)(2,1)S(1)} %get-tuple-element.23), channel_id=1, source_target_pairs={{0,30},{2,0},{4,2},{6,4},{8,6},{10,8},{12,10},{14,12},{16,14},{18,... | collective-permute-start | bytes 73736 | tf_op jit(solution)/shard_map/ppermute | solution.py:38
  31.1 7.2 %fine.1 = (f32[208,256]{1,0:T(8,128)S(1)}, bf16[9,9,256,128]{3,2,1,0:T(8,128)(2,1)S(1)}) custom-call(f32[40,48,128]{2,1,0:T(8,128)S(1)} %get-tuple-element.24.fine_ref, f32[17,24,128]{2,1,0:T(8,128)S(1)} %get-tuple-element.25.row_ref, f32[18,24,128]{2,1,0:T(8,128)S(1)} %get-tuple-element.26.coarse_row_ref), custom_call_target="tpu_custom_call" | custom-call | tf_op jit(solution)/shard_map/fine/pallas_call | solution.py:430
  38.2 0.0 collective-permute-done.5.refs_1_
  38.2 0.0 collective-permute-done.6.refs_2_
  38.3 3.9 %coarse.1 = (f32[16,16,128]{2,1,0:T(8,128)}, bf16[376,256]{1,0:T(8,128)(2,1)S(1)}) custom-call(bf16[16,16,128]{2,1,0:T(8,128)(2,1)S(1)} %get-tuple-element.21.refs_0_, bf16[6,16,128]{2,1,0:T(8,128)(2,1)S(1)} %collective-permute-done.5.refs_1_, bf16[6,16,128]{2,1,0:T(8,128)(2,1)S(1)} %collective-permute-done.6.refs_2_, ...), custom_call_target="tpu_custom_call" | custom-call | tf_op jit(solution)/shard_map/coarse/pallas_call | solution.py:573
  42.2 5.5 %read.1 = f32[1,1,16384]{2,1,0:T(1,128)} custom-call(s32[1,1]{1,0:T(1,128)S(6)} %copy.8.count_ref, bf16[376,256]{1,0:T(8,128)(2,1)S(1)} %get-tuple-element.29.grid_ref, bf16[128,16384]{1,0:T(8,128)(2,1)S(1)} %get-tuple-element.30.depth_ref, f32[24,16384]{1,0:T(8,128)S(1)} %get-tuple-element.31.first_ref, f32[24,16384]{1,0:T(8,128)S(1)} %get-tuple-element.32.second_ref), custom_call_target="tpu_custom_call" | custom-call | tf_op jit(solution)/shard_map/read/pallas_call | solution.py:220
Async XLA Ops:
  12.7 10.7 %collective-permute-start = (f32[11,24,128]{2,1,0:T(8,128)S(1)}, f32[11,24,128]{2,1,0:T(8,128)S(1)}, u32[]{:S(2)}, u32[]{:S(2)}) collective-permute-start(f32[11,24,128]{2,1,0:T(8,128)S(1)} %get-tuple-element.19), channel_id=1, source_target_pairs={{0,2},{2,4},{4,6},{6,8},{8,10},{10,12},{12,14},{14,16},{16,18},{18... | collective-permute-start | bytes 405512 | tf_op jit(solution)/shard_map/ppermute | solution.py:38
  15.7 7.7 %collective-permute-start.1 = (f32[11,24,128]{2,1,0:T(8,128)S(1)}, f32[11,24,128]{2,1,0:T(8,128)S(1)}, u32[]{:S(2)}, u32[]{:S(2)}) collective-permute-start(f32[11,24,128]{2,1,0:T(8,128)S(1)} %get-tuple-element.20), channel_id=1, source_target_pairs={{0,30},{2,0},{4,2},{6,4},{8,6},{10,8},{12,10},{14,12},{16,14},{18,... | collective-permute-start | bytes 405512 | tf_op jit(solution)/shard_map/ppermute | solution.py:38
  19.7 4.1 %collective-permute-start.2 = (f32[456,128]{1,0:T(8,128)S(1)}, f32[456,128]{1,0:T(8,128)S(1)}, u32[]{:S(2)}, u32[]{:S(2)}) collective-permute-start(f32[456,128]{1,0:T(8,128)S(1)} %get-tuple-element.18.refs_0_), channel_id=1, source_target_pairs={{0,1},{1,0},{2,3},{3,2},{4,5},{5,4},{6,7},{7,6},{8,9},{9,8},{10,11... | collective-permute-start | bytes 700424 | tf_op jit(solution)/shard_map/ppermute | solution.py:38
  23.4 1.4 %collective-permute-start.3 = (f32[11,24,128]{2,1,0:T(8,128)S(1)}, f32[11,24,128]{2,1,0:T(8,128)S(1)}, u32[]{:S(2)}, u32[]{:S(2)}) collective-permute-start(f32[11,24,128]{2,1,0:T(8,128)S(1)} %collective-permute-done.refs_1_), channel_id=1, source_target_pairs={{0,1},{1,0},{2,3},{3,2},{4,5},{5,4},{6,7},{7,6},{8,9},{9,8},{10,11... | collective-permute-start | bytes 405512 | tf_op jit(solution)/shard_map/ppermute | solution.py:38
  23.4 1.5 %collective-permute-start.4 = (f32[11,24,128]{2,1,0:T(8,128)S(1)}, f32[11,24,128]{2,1,0:T(8,128)S(1)}, u32[]{:S(2)}, u32[]{:S(2)}) collective-permute-start(f32[11,24,128]{2,1,0:T(8,128)S(1)} %collective-permute-done.1.refs_2_), channel_id=1, source_target_pairs={{0,1},{1,0},{2,3},{3,2},{4,5},{5,4},{6,7},{7,6},{8,9},{9,8},{10,11... | collective-permute-start | bytes 405512 | tf_op jit(solution)/shard_map/ppermute | solution.py:38
  25.4 12.8 %collective-permute-start.5 = (bf16[6,16,128]{2,1,0:T(8,128)(2,1)S(1)}, bf16[6,16,128]{2,1,0:T(8,128)(2,1)S(1)}, u32[]{:S(2)}, u32[]{:S(2)}) collective-permute-start(bf16[6,16,128]{2,1,0:T(8,128)(2,1)S(1)} %get-tuple-element.22), channel_id=1, source_target_pairs={{0,2},{2,4},{4,6},{6,8},{8,10},{10,12},{12,14},{14,16},{16,18},{18... | collective-permute-start | bytes 73736 | tf_op jit(solution)/shard_map/ppermute | solution.py:38
  26.8 11.5 %collective-permute-start.6 = (bf16[6,16,128]{2,1,0:T(8,128)(2,1)S(1)}, bf16[6,16,128]{2,1,0:T(8,128)(2,1)S(1)}, u32[]{:S(2)}, u32[]{:S(2)}) collective-permute-start(bf16[6,16,128]{2,1,0:T(8,128)(2,1)S(1)} %get-tuple-element.23), channel_id=1, source_target_pairs={{0,30},{2,0},{4,2},{6,4},{8,6},{10,8},{12,10},{14,12},{16,14},{18,... | collective-permute-start | bytes 73736 | tf_op jit(solution)/shard_map/ppermute | solution.py:38

commit v3 on v2

--- a/solution.py
+++ b/solution.py
@@ -12,9 +12,10 @@
 
 SPAN = LX + 3
 SPAN_PAD = 24
-BLOCK = 2048
+BLOCK = 4096
 CHUNK = 256
 READ_CHUNK = 512
+READ_BLOCK = 8192
 FACE = SPAN * LY + (SPAN - LY) * SPAN_PAD
 VMEM_BYTES = 24 * 1024 * 1024
 REACH = 11
@@ -145,9 +146,9 @@
 
 def read_kernel(count_ref, grid_ref, depth_ref, first_ref, second_ref, out_ref):
     step = pl.program_id(0)
-    for start in range(0, BLOCK, READ_CHUNK):
+    for start in range(0, READ_BLOCK, READ_CHUNK):
         beads = slice(start, start + READ_CHUNK)
-        kept = pl.ds(pl.multiple_of(step * BLOCK, BLOCK) + start, READ_CHUNK)
+        kept = pl.ds(pl.multiple_of(step * READ_BLOCK, READ_BLOCK) + start, READ_CHUNK)
         depth = depth_ref[:, kept]
         along = jnp.dot(
             grid_ref[...],
@@ -169,7 +170,7 @@
         parts = [inside[row : row + 8] for row in range(0, LY, 8)]
         parts += [outside[row : row + 8] for row in range(0, SPAN_PAD, 8)]
         picked = jnp.sum(sum(parts[1:], parts[0]), axis=0, keepdims=True)
-        slots = lax.broadcasted_iota(jnp.int32, picked.shape, 1) + (step * BLOCK + start)
+        slots = lax.broadcasted_iota(jnp.int32, picked.shape, 1) + (step * READ_BLOCK + start)
         out_ref[0, :, beads] = jnp.where(slots < count_ref[0, 0], picked, 0.0)
 
 
@@ -219,9 +220,13 @@
     slots = tables[0].shape[1]
     return pl.pallas_call(
         read_kernel,
-        grid=(slots // BLOCK,),
-        in_specs=[pl.BlockSpec(memory_space=pltpu.SMEM), whole_spec(grid.shape)] + table_specs(),
-        out_specs=pl.BlockSpec((1, 1, BLOCK), lambda i: (0, 0, i)),
+        grid=(slots // READ_BLOCK,),
+        in_specs=[
+            pl.BlockSpec(memory_space=pltpu.SMEM),
+            pl.BlockSpec(memory_space=pltpu.VMEM),
+        ]
+        + table_specs(),
+        out_specs=pl.BlockSpec((1, 1, READ_BLOCK), lambda i: (0, 0, i)),
         out_shape=jax.ShapeDtypeStruct((1, 1, slots), jnp.float32),
         name="read",
         compiler_params=pltpu.CompilerParams(vmem_limit_bytes=VMEM_BYTES),
@@ -455,16 +460,11 @@
     face_ref,
     cell_ref,
     pair_ref,
-    total_ref,
     coarse_ref,
     wide_ref,
     join_ref,
 ):
-    step = pl.program_id(0)
-
-    @pl.when(step == 0)
-    def _():
-        total_ref[...] = jnp.zeros_like(total_ref)
+    def prepare():
         cell_ref[...] = jnp.zeros_like(cell_ref)
         for start, part in ((0, below_ref), (EDGE, own_ref), (EDGE + KNOWN, above_ref)):
             planes = slice(start, start + part.shape[0])
@@ -488,16 +488,17 @@
                 [pair[:COARSE_IN].reshape(rows, LZ), pair[1:].reshape(rows, LZ)], axis=1
             ).astype(jnp.bfloat16)
 
-    rows = pl.ds(pl.multiple_of(step * 16, 16), COARSE_OUT * 8)
-    total = total_ref[...]
-    for shift in range(SHIFTS):
-        total = total + jnp.dot(
-            pair_ref[shift, rows], table_ref[0, shift], preferred_element_type=jnp.float32
-        )
-    total_ref[...] = total
-
-    @pl.when(step == pl.num_programs(0) - 1)
-    def _():
+    prepare()
+    total = None
+    for pair in range(table_ref.shape[0]):
+        rows = slice(pair * 16, pair * 16 + COARSE_OUT * 8)
+        for shift in range(SHIFTS):
+            part = jnp.dot(
+                pair_ref[shift, rows], table_ref[pair, shift], preferred_element_type=jnp.float32
+            )
+            total = part if total is None else total + part
+
+    def finish():
         high = total.astype(jnp.bfloat16)
         low = (total - high.astype(jnp.float32)).astype(jnp.bfloat16)
         shape = (2 * LZ, 2 * LZ)
@@ -555,15 +556,12 @@
         face_ref[:, :LZ] = face_high
         face_ref[:, LZ:] = face_low
 
+    finish()
+
 
 def potentials(own, below, above, low, high, table, sums):
-    def whole(value):
-        return pl.BlockSpec(value.shape, lambda i: (0,) * value.ndim)
-
     given = [own, below, above] + ([] if low is None else [low, high])
-    specs = [whole(value) for value in given]
-    specs.append(pl.BlockSpec((1, SHIFTS, 2 * LZ, LZ), lambda i: (i, 0, 0, 0)))
-    specs.append(whole(sums))
+    specs = [pl.BlockSpec(memory_space=pltpu.VMEM)] * (len(given) + 2)
 
     def body(*refs):
         if low is None:
@@ -572,12 +570,7 @@
 
     return pl.pallas_call(
         body,
-        grid=(table.shape[0],),
         in_specs=specs,
-        out_specs=(
-            pl.BlockSpec((LX, LY, LZ), lambda i: (0, 0, 0)),
-            pl.BlockSpec((FACE, 2 * LZ), lambda i: (0, 0)),
-        ),
         out_shape=(
             jax.ShapeDtypeStruct((LX, LY, LZ), jnp.float32),
             jax.ShapeDtypeStruct((FACE, 2 * LZ), jnp.bfloat16),
@@ -585,7 +578,6 @@
         scratch_shapes=[
             pltpu.VMEM((COARSE_IN + 1, 40, LZ), jnp.float32),
             pltpu.VMEM((SHIFTS, COARSE_IN * 8, 2 * LZ), jnp.bfloat16),
-            pltpu.VMEM((COARSE_OUT * 8, LZ), jnp.float32),
             pltpu.VMEM((COARSE_OUT, 16, LZ), jnp.float32),
             pltpu.VMEM((SPAN, 24, LZ), jnp.float32),
             pltpu.VMEM((SPAN_PAD * 32, LZ), jnp.float32),

time: 47.8 us -> 44.4 us (0.929)
  Pallas kernels: 28.4 us -> 25 us
    pallas_call x2, Pallas kernels: 9.38 us -> 6.69 us  [the longest x1 4.48 us: read_beads(): pl.pallas_call(read_kernel, grid=(slots // READ_BLOCK,), in_specs=[pl.Blo...]
    pallas_call x1, Pallas kernels: 11.4 us -> 10.7 us  [spread_beads(): pl.pallas_call(spread_kernel, grid=(slots // BLOCK,), in_specs=[pl.BlockS...]
  transfers between devices with their start and end apart: 7 -> 7, of which waited for: 3 -> 3; matrix products, arithmetic and copies ran while one was open for 0% -> 0% of each run, Pallas kernels for 15% -> 16%
where the time goes in v3:
time: 44.4 us; the launch traced here: 44.2 us
  Pallas kernels  25 us (56%)
  starting transfers between devices  13.3 us (30%)
  waiting for transfers between devices  4.62 us (10%)
  between operations  1.32 us (3%)
    ppermute x7, starting transfers between devices, from_behind(): return lax.ppermute(value, axis, pairs)  13.3 us
    pallas_call x1, Pallas kernels, spread_beads(): pl.pallas_call(spread_kernel, grid=(slots // BLOCK,), in_specs=[pl.BlockS...  10.7 us
    pallas_call x1, Pallas kernels, fine_sums(): pl.pallas_call(fine_kernel, out_shape=(jax.ShapeDtypeStruct((NEAR + FAR,...  7.15 us
    ppermute x7, waiting for transfers between devices, from_behind(): return lax.ppermute(value, axis, pairs)  4.62 us
    pallas_call x1, Pallas kernels, read_beads(): pl.pallas_call(read_kernel, grid=(slots // READ_BLOCK,), in_specs=[pl.Blo...  4.48 us
    pallas_call x1, Pallas kernels, potentials(): pl.pallas_call(body, in_specs=specs, out_shape=(jax.ShapeDtypeStruct((LX,...  2.22 us
  transfers between devices with their start and end apart: 7, of which 3 were waited for; matrix products, arithmetic and copies ran while one was open for 0% of the time, Pallas kernels for 16%

profile of v3, /device:TPU:0, one launch (start us, length us, event | category | flops | bytes accessed | tf_op | source)
XLA Modules:
  0.0 44.2 jit_solution(8875340818574986153)
XLA Ops:
  1.3 10.7 %spread.1 = (f32[456,128]{1,0:T(8,128)S(1)}, f32[11,24,128]{2,1,0:T(8,128)S(1)}, f32[11,24,128]{2,1,0:T(8,128)S(1)}, bf16[128,16384]{1,0:T(8,128)(2,1)S(1)}, f32...) custom-call(s32[1,1]{1,0:T(1,128)S(6)} %copy.8.count_ref, ...), custom_call_target="tpu_custom_call" | custom-call | tf_op jit(solution)/shard_map/spread/pallas_call | solution.py:202
  11.9 3.0 %collective-permute-start = (f32[11,24,128]{2,1,0:T(8,128)S(1)}, f32[11,24,128]{2,1,0:T(8,128)S(1)}, u32[]{:S(2)}, u32[]{:S(2)}) collective-permute-start(f32[11,24,128]{2,1,0:T(8,128)S(1)} %get-tuple-element.19), channel_id=1, source_target_pairs={{0,2},{2,4},{4,6},{6,8},{8,10},{10,12},{12,14},{14,16},{16,18},{18... | collective-permute-start | bytes 405512 | tf_op jit(solution)/shard_map/ppermute | solution.py:39
  15.0 4.1 %collective-permute-start.1 = (f32[11,24,128]{2,1,0:T(8,128)S(1)}, f32[11,24,128]{2,1,0:T(8,128)S(1)}, u32[]{:S(2)}, u32[]{:S(2)}) collective-permute-start(f32[11,24,128]{2,1,0:T(8,128)S(1)} %get-tuple-element.20), channel_id=1, source_target_pairs={{0,30},{2,0},{4,2},{6,4},{8,6},{10,8},{12,10},{14,12},{16,14},{18,... | collective-permute-start | bytes 405512 | tf_op jit(solution)/shard_map/ppermute | solution.py:39
  19.1 0.0 collective-permute-start.2
  19.1 3.6 %collective-permute-done.refs_1_ = f32[11,24,128]{2,1,0:T(8,128)S(1)} collective-permute-done((f32[11,24,128]{2,1,0:T(8,128)S(1)}, f32[11,24,128]{2,1,0:T(8,128)S(1)}, u32[]{:S(2)}, u32[]{:S(2)}) %collective-permute-start) | collective-permute-done | bytes 135200 | tf_op jit(solution)/shard_map/ppermute | solution.py:39
  22.6 0.0 collective-permute-start.3
  22.6 0.0 collective-permute-done.1.refs_2_
  22.7 0.5 %collective-permute-start.4 = (f32[11,24,128]{2,1,0:T(8,128)S(1)}, f32[11,24,128]{2,1,0:T(8,128)S(1)}, u32[]{:S(2)}, u32[]{:S(2)}) collective-permute-start(f32[11,24,128]{2,1,0:T(8,128)S(1)} %collective-permute-done.1.refs_2_), channel_id=1, source_target_pairs={{0,1},{1,0},{2,3},{3,2},{4,5},{5,4},{6,7},{7,6},{8,9},{9,8},{10,11... | collective-permute-start | bytes 405512 | tf_op jit(solution)/shard_map/ppermute | solution.py:39
  23.2 0.0 collective-permute-done.2.refs_3_
  23.2 0.8 %collective-permute-done.3.refs_4_ = f32[11,24,128]{2,1,0:T(8,128)S(1)} collective-permute-done((f32[11,24,128]{2,1,0:T(8,128)S(1)}, f32[11,24,128]{2,1,0:T(8,128)S(1)}, u32[]{:S(2)}, u32[]{:S(2)}) %collective-permute-start.3) | collective-permute-done | bytes 135200 | tf_op jit(solution)/shard_map/ppermute | solution.py:39
  24.0 0.2 collective-permute-done.4.refs_5_
  24.2 0.5 %gather.1 = (f32[40,48,128]{2,1,0:T(8,128)S(1)}, bf16[16,16,128]{2,1,0:T(8,128)(2,1)S(1)}, bf16[6,16,128]{2,1,0:T(8,128)(2,1)S(1)}, bf16[6,16,128]{2,1,0:T(8,128)(2,1)S(1)}) custom-call(f32[456,128]{1,0:T(8,128)S(1)} %get-tuple-element.18.refs_0_, f32[11,24,128]{2,1,0:T(8,128)S(1)} %collective-permute-done.refs_1_, ...), custom_call_target="tpu_custom_call" | custom-call | tf_op jit(solution)/shard_map/gather/pallas_call | solution.py:336
  24.7 1.4 %collective-permute-start.5 = (bf16[6,16,128]{2,1,0:T(8,128)(2,1)S(1)}, bf16[6,16,128]{2,1,0:T(8,128)(2,1)S(1)}, u32[]{:S(2)}, u32[]{:S(2)}) collective-permute-start(bf16[6,16,128]{2,1,0:T(8,128)(2,1)S(1)} %get-tuple-element.22), channel_id=1, source_target_pairs={{0,2},{2,4},{4,6},{6,8},{8,10},{10,12},{12,14},{14,16},{16,18},{18... | collective-permute-start | bytes 73736 | tf_op jit(solution)/shard_map/ppermute | solution.py:39
  26.1 4.3 %collective-permute-start.6 = (bf16[6,16,128]{2,1,0:T(8,128)(2,1)S(1)}, bf16[6,16,128]{2,1,0:T(8,128)(2,1)S(1)}, u32[]{:S(2)}, u32[]{:S(2)}) collective-permute-start(bf16[6,16,128]{2,1,0:T(8,128)(2,1)S(1)} %get-tuple-element.23), channel_id=1, source_target_pairs={{0,30},{2,0},{4,2},{6,4},{8,6},{10,8},{12,10},{14,12},{16,14},{18,... | collective-permute-start | bytes 73736 | tf_op jit(solution)/shard_map/ppermute | solution.py:39
  30.3 7.2 %fine.1 = (f32[208,256]{1,0:T(8,128)S(1)}, bf16[9,9,256,128]{3,2,1,0:T(8,128)(2,1)S(1)}) custom-call(f32[40,48,128]{2,1,0:T(8,128)S(1)} %get-tuple-element.24.fine_ref, f32[17,24,128]{2,1,0:T(8,128)S(1)} %get-tuple-element.25.row_ref, f32[18,24,128]{2,1,0:T(8,128)S(1)} %get-tuple-element.26.coarse_row_ref), custom_call_target="tpu_custom_call" | custom-call | tf_op jit(solution)/shard_map/fine/pallas_call | solution.py:435
  37.5 0.0 collective-permute-done.5.refs_1_
  37.5 0.0 collective-permute-done.6.refs_2_
  37.5 2.2 %coarse.1 = (f32[16,16,128]{2,1,0:T(8,128)}, bf16[376,256]{1,0:T(8,128)(2,1)S(1)}) custom-call(bf16[16,16,128]{2,1,0:T(8,128)(2,1)S(1)} %get-tuple-element.21.refs_0_, bf16[6,16,128]{2,1,0:T(8,128)(2,1)S(1)} %collective-permute-done.5.refs_1_, bf16[6,16,128]{2,1,0:T(8,128)(2,1)S(1)} %collective-permute-done.6.refs_2_, ...), custom_call_target="tpu_custom_call" | custom-call | tf_op jit(solution)/shard_map/coarse/pallas_call | solution.py:571
  39.7 4.5 %read.1 = f32[1,1,16384]{2,1,0:T(1,128)} custom-call(s32[1,1]{1,0:T(1,128)S(6)} %copy.8.count_ref, bf16[376,256]{1,0:T(8,128)(2,1)S(1)} %get-tuple-element.29.grid_ref, bf16[128,16384]{1,0:T(8,128)(2,1)S(1)} %get-tuple-element.30.depth_ref, f32[24,16384]{1,0:T(8,128)S(1)} %get-tuple-element.31.first_ref, f32[24,16384]{1,0:T(8,128)S(1)} %get-tuple-element.32.second_ref), custom_call_target="tpu_custom_call" | custom-call | tf_op jit(solution)/shard_map/read/pallas_call | solution.py:221
Async XLA Ops:
  11.9 10.7 %collective-permute-start = (f32[11,24,128]{2,1,0:T(8,128)S(1)}, f32[11,24,128]{2,1,0:T(8,128)S(1)}, u32[]{:S(2)}, u32[]{:S(2)}) collective-permute-start(f32[11,24,128]{2,1,0:T(8,128)S(1)} %get-tuple-element.19), channel_id=1, source_target_pairs={{0,2},{2,4},{4,6},{6,8},{8,10},{10,12},{12,14},{14,16},{16,18},{18... | collective-permute-start | bytes 405512 | tf_op jit(solution)/shard_map/ppermute | solution.py:39
  15.0 7.7 %collective-permute-start.1 = (f32[11,24,128]{2,1,0:T(8,128)S(1)}, f32[11,24,128]{2,1,0:T(8,128)S(1)}, u32[]{:S(2)}, u32[]{:S(2)}) collective-permute-start(f32[11,24,128]{2,1,0:T(8,128)S(1)} %get-tuple-element.20), channel_id=1, source_target_pairs={{0,30},{2,0},{4,2},{6,4},{8,6},{10,8},{12,10},{14,12},{16,14},{18,... | collective-permute-start | bytes 405512 | tf_op jit(solution)/shard_map/ppermute | solution.py:39
  19.1 4.1 %collective-permute-start.2 = (f32[456,128]{1,0:T(8,128)S(1)}, f32[456,128]{1,0:T(8,128)S(1)}, u32[]{:S(2)}, u32[]{:S(2)}) collective-permute-start(f32[456,128]{1,0:T(8,128)S(1)} %get-tuple-element.18.refs_0_), channel_id=1, source_target_pairs={{0,1},{1,0},{2,3},{3,2},{4,5},{5,4},{6,7},{7,6},{8,9},{9,8},{10,11... | collective-permute-start | bytes 700424 | tf_op jit(solution)/shard_map/ppermute | solution.py:39
  22.6 1.4 %collective-permute-start.3 = (f32[11,24,128]{2,1,0:T(8,128)S(1)}, f32[11,24,128]{2,1,0:T(8,128)S(1)}, u32[]{:S(2)}, u32[]{:S(2)}) collective-permute-start(f32[11,24,128]{2,1,0:T(8,128)S(1)} %collective-permute-done.refs_1_), channel_id=1, source_target_pairs={{0,1},{1,0},{2,3},{3,2},{4,5},{5,4},{6,7},{7,6},{8,9},{9,8},{10,11... | collective-permute-start | bytes 405512 | tf_op jit(solution)/shard_map/ppermute | solution.py:39
  22.7 1.5 %collective-permute-start.4 = (f32[11,24,128]{2,1,0:T(8,128)S(1)}, f32[11,24,128]{2,1,0:T(8,128)S(1)}, u32[]{:S(2)}, u32[]{:S(2)}) collective-permute-start(f32[11,24,128]{2,1,0:T(8,128)S(1)} %collective-permute-done.1.refs_2_), channel_id=1, source_target_pairs={{0,1},{1,0},{2,3},{3,2},{4,5},{5,4},{6,7},{7,6},{8,9},{9,8},{10,11... | collective-permute-start | bytes 405512 | tf_op jit(solution)/shard_map/ppermute | solution.py:39
  24.7 12.8 %collective-permute-start.5 = (bf16[6,16,128]{2,1,0:T(8,128)(2,1)S(1)}, bf16[6,16,128]{2,1,0:T(8,128)(2,1)S(1)}, u32[]{:S(2)}, u32[]{:S(2)}) collective-permute-start(bf16[6,16,128]{2,1,0:T(8,128)(2,1)S(1)} %get-tuple-element.22), channel_id=1, source_target_pairs={{0,2},{2,4},{4,6},{6,8},{8,10},{10,12},{12,14},{14,16},{16,18},{18... | collective-permute-start | bytes 73736 | tf_op jit(solution)/shard_map/ppermute | solution.py:39
  26.1 11.4 %collective-permute-start.6 = (bf16[6,16,128]{2,1,0:T(8,128)(2,1)S(1)}, bf16[6,16,128]{2,1,0:T(8,128)(2,1)S(1)}, u32[]{:S(2)}, u32[]{:S(2)}) collective-permute-start(bf16[6,16,128]{2,1,0:T(8,128)(2,1)S(1)} %get-tuple-element.23), channel_id=1, source_target_pairs={{0,30},{2,0},{4,2},{6,4},{8,6},{10,8},{12,10},{14,12},{16,14},{18,... | collective-permute-start | bytes 73736 | tf_op jit(solution)/shard_map/ppermute | solution.py:39

commit v4 on v3

--- a/solution.py
+++ b/solution.py
@@ -12,7 +12,7 @@
 
 SPAN = LX + 3
 SPAN_PAD = 24
-BLOCK = 4096
+BLOCK = 8192
 CHUNK = 256
 READ_CHUNK = 512
 READ_BLOCK = 8192

time: 44.4 us -> 44 us (level)
  no operation moved by 1% of the time
where the time goes in v4:
time: 44 us; the launch traced here: 43.9 us
  Pallas kernels  24.6 us (56%)
  starting transfers between devices  13.3 us (30%)
  waiting for transfers between devices  4.66 us (11%)
  between operations  1.32 us (3%)
    ppermute x7, starting transfers between devices, from_behind(): return lax.ppermute(value, axis, pairs)  13.3 us
    pallas_call x1, Pallas kernels, spread_beads(): pl.pallas_call(spread_kernel, grid=(slots // BLOCK,), in_specs=[pl.BlockS...  10.3 us
    pallas_call x1, Pallas kernels, fine_sums(): pl.pallas_call(fine_kernel, out_shape=(jax.ShapeDtypeStruct((NEAR + FAR,...  7.15 us
    ppermute x7, waiting for transfers between devices, from_behind(): return lax.ppermute(value, axis, pairs)  4.66 us
    pallas_call x1, Pallas kernels, read_beads(): pl.pallas_call(read_kernel, grid=(slots // READ_BLOCK,), in_specs=[pl.Blo...  4.48 us
    pallas_call x1, Pallas kernels, potentials(): pl.pallas_call(body, in_specs=specs, out_shape=(jax.ShapeDtypeStruct((LX,...  2.21 us
  transfers between devices with their start and end apart: 7, of which 3 were waited for; matrix products, arithmetic and copies ran while one was open for 0% of the time, Pallas kernels for 16%

profile of v4, /device:TPU:0, one launch (start us, length us, event | category | flops | bytes accessed | tf_op | source)
XLA Modules:
  0.0 43.9 jit_solution(13124443540996743337)
XLA Ops:
  1.3 10.3 %spread.1 = (f32[456,128]{1,0:T(8,128)S(1)}, f32[11,24,128]{2,1,0:T(8,128)S(1)}, f32[11,24,128]{2,1,0:T(8,128)S(1)}, bf16[128,16384]{1,0:T(8,128)(2,1)S(1)}, f32...) custom-call(s32[1,1]{1,0:T(1,128)S(6)} %copy.8.count_ref, ...), custom_call_target="tpu_custom_call" | custom-call | tf_op jit(solution)/shard_map/spread/pallas_call | solution.py:202
  11.6 3.0 %collective-permute-start = (f32[11,24,128]{2,1,0:T(8,128)S(1)}, f32[11,24,128]{2,1,0:T(8,128)S(1)}, u32[]{:S(2)}, u32[]{:S(2)}) collective-permute-start(f32[11,24,128]{2,1,0:T(8,128)S(1)} %get-tuple-element.19), channel_id=1, source_target_pairs={{0,2},{2,4},{4,6},{6,8},{8,10},{10,12},{12,14},{14,16},{16,18},{18... | collective-permute-start | bytes 405512 | tf_op jit(solution)/shard_map/ppermute | solution.py:39
  14.6 4.1 %collective-permute-start.1 = (f32[11,24,128]{2,1,0:T(8,128)S(1)}, f32[11,24,128]{2,1,0:T(8,128)S(1)}, u32[]{:S(2)}, u32[]{:S(2)}) collective-permute-start(f32[11,24,128]{2,1,0:T(8,128)S(1)} %get-tuple-element.20), channel_id=1, source_target_pairs={{0,30},{2,0},{4,2},{6,4},{8,6},{10,8},{12,10},{14,12},{16,14},{18,... | collective-permute-start | bytes 405512 | tf_op jit(solution)/shard_map/ppermute | solution.py:39
  18.7 0.0 collective-permute-start.2
  18.7 3.6 %collective-permute-done.refs_1_ = f32[11,24,128]{2,1,0:T(8,128)S(1)} collective-permute-done((f32[11,24,128]{2,1,0:T(8,128)S(1)}, f32[11,24,128]{2,1,0:T(8,128)S(1)}, u32[]{:S(2)}, u32[]{:S(2)}) %collective-permute-start) | collective-permute-done | bytes 135200 | tf_op jit(solution)/shard_map/ppermute | solution.py:39
  22.3 0.0 collective-permute-start.3
  22.3 0.0 collective-permute-done.1.refs_2_
  22.3 0.5 %collective-permute-start.4 = (f32[11,24,128]{2,1,0:T(8,128)S(1)}, f32[11,24,128]{2,1,0:T(8,128)S(1)}, u32[]{:S(2)}, u32[]{:S(2)}) collective-permute-start(f32[11,24,128]{2,1,0:T(8,128)S(1)} %collective-permute-done.1.refs_2_), channel_id=1, source_target_pairs={{0,1},{1,0},{2,3},{3,2},{4,5},{5,4},{6,7},{7,6},{8,9},{9,8},{10,11... | collective-permute-start | bytes 405512 | tf_op jit(solution)/shard_map/ppermute | solution.py:39
  22.8 0.0 collective-permute-done.2.refs_3_
  22.8 0.8 %collective-permute-done.3.refs_4_ = f32[11,24,128]{2,1,0:T(8,128)S(1)} collective-permute-done((f32[11,24,128]{2,1,0:T(8,128)S(1)}, f32[11,24,128]{2,1,0:T(8,128)S(1)}, u32[]{:S(2)}, u32[]{:S(2)}) %collective-permute-start.3) | collective-permute-done | bytes 135200 | tf_op jit(solution)/shard_map/ppermute | solution.py:39
  23.7 0.2 collective-permute-done.4.refs_5_
  23.9 0.5 %gather.1 = (f32[40,48,128]{2,1,0:T(8,128)S(1)}, bf16[16,16,128]{2,1,0:T(8,128)(2,1)S(1)}, bf16[6,16,128]{2,1,0:T(8,128)(2,1)S(1)}, bf16[6,16,128]{2,1,0:T(8,128)(2,1)S(1)}) custom-call(f32[456,128]{1,0:T(8,128)S(1)} %get-tuple-element.18.refs_0_, f32[11,24,128]{2,1,0:T(8,128)S(1)} %collective-permute-done.refs_1_, ...), custom_call_target="tpu_custom_call" | custom-call | tf_op jit(solution)/shard_map/gather/pallas_call | solution.py:336
  24.3 1.4 %collective-permute-start.5 = (bf16[6,16,128]{2,1,0:T(8,128)(2,1)S(1)}, bf16[6,16,128]{2,1,0:T(8,128)(2,1)S(1)}, u32[]{:S(2)}, u32[]{:S(2)}) collective-permute-start(bf16[6,16,128]{2,1,0:T(8,128)(2,1)S(1)} %get-tuple-element.22), channel_id=1, source_target_pairs={{0,2},{2,4},{4,6},{6,8},{8,10},{10,12},{12,14},{14,16},{16,18},{18... | collective-permute-start | bytes 73736 | tf_op jit(solution)/shard_map/ppermute | solution.py:39
  25.7 4.3 %collective-permute-start.6 = (bf16[6,16,128]{2,1,0:T(8,128)(2,1)S(1)}, bf16[6,16,128]{2,1,0:T(8,128)(2,1)S(1)}, u32[]{:S(2)}, u32[]{:S(2)}) collective-permute-start(bf16[6,16,128]{2,1,0:T(8,128)(2,1)S(1)} %get-tuple-element.23), channel_id=1, source_target_pairs={{0,30},{2,0},{4,2},{6,4},{8,6},{10,8},{12,10},{14,12},{16,14},{18,... | collective-permute-start | bytes 73736 | tf_op jit(solution)/shard_map/ppermute | solution.py:39
  30.0 7.1 %fine.1 = (f32[208,256]{1,0:T(8,128)S(1)}, bf16[9,9,256,128]{3,2,1,0:T(8,128)(2,1)S(1)}) custom-call(f32[40,48,128]{2,1,0:T(8,128)S(1)} %get-tuple-element.24.fine_ref, f32[17,24,128]{2,1,0:T(8,128)S(1)} %get-tuple-element.25.row_ref, f32[18,24,128]{2,1,0:T(8,128)S(1)} %get-tuple-element.26.coarse_row_ref), custom_call_target="tpu_custom_call" | custom-call | tf_op jit(solution)/shard_map/fine/pallas_call | solution.py:435
  37.2 0.0 collective-permute-done.5.refs_1_
  37.2 0.0 collective-permute-done.6.refs_2_
  37.2 2.2 %coarse.1 = (f32[16,16,128]{2,1,0:T(8,128)}, bf16[376,256]{1,0:T(8,128)(2,1)S(1)}) custom-call(bf16[16,16,128]{2,1,0:T(8,128)(2,1)S(1)} %get-tuple-element.21.refs_0_, bf16[6,16,128]{2,1,0:T(8,128)(2,1)S(1)} %collective-permute-done.5.refs_1_, bf16[6,16,128]{2,1,0:T(8,128)(2,1)S(1)} %collective-permute-done.6.refs_2_, ...), custom_call_target="tpu_custom_call" | custom-call | tf_op jit(solution)/shard_map/coarse/pallas_call | solution.py:571
  39.4 4.5 %read.1 = f32[1,1,16384]{2,1,0:T(1,128)} custom-call(s32[1,1]{1,0:T(1,128)S(6)} %copy.8.count_ref, bf16[376,256]{1,0:T(8,128)(2,1)S(1)} %get-tuple-element.29.grid_ref, bf16[128,16384]{1,0:T(8,128)(2,1)S(1)} %get-tuple-element.30.depth_ref, f32[24,16384]{1,0:T(8,128)S(1)} %get-tuple-element.31.first_ref, f32[24,16384]{1,0:T(8,128)S(1)} %get-tuple-element.32.second_ref), custom_call_target="tpu_custom_call" | custom-call | tf_op jit(solution)/shard_map/read/pallas_call | solution.py:221
Async XLA Ops:
  11.6 10.7 %collective-permute-start = (f32[11,24,128]{2,1,0:T(8,128)S(1)}, f32[11,24,128]{2,1,0:T(8,128)S(1)}, u32[]{:S(2)}, u32[]{:S(2)}) collective-permute-start(f32[11,24,128]{2,1,0:T(8,128)S(1)} %get-tuple-element.19), channel_id=1, source_target_pairs={{0,2},{2,4},{4,6},{6,8},{8,10},{10,12},{12,14},{14,16},{16,18},{18... | collective-permute-start | bytes 405512 | tf_op jit(solution)/shard_map/ppermute | solution.py:39
  14.6 7.7 %collective-permute-start.1 = (f32[11,24,128]{2,1,0:T(8,128)S(1)}, f32[11,24,128]{2,1,0:T(8,128)S(1)}, u32[]{:S(2)}, u32[]{:S(2)}) collective-permute-start(f32[11,24,128]{2,1,0:T(8,128)S(1)} %get-tuple-element.20), channel_id=1, source_target_pairs={{0,30},{2,0},{4,2},{6,4},{8,6},{10,8},{12,10},{14,12},{16,14},{18,... | collective-permute-start | bytes 405512 | tf_op jit(solution)/shard_map/ppermute | solution.py:39
  18.7 4.1 %collective-permute-start.2 = (f32[456,128]{1,0:T(8,128)S(1)}, f32[456,128]{1,0:T(8,128)S(1)}, u32[]{:S(2)}, u32[]{:S(2)}) collective-permute-start(f32[456,128]{1,0:T(8,128)S(1)} %get-tuple-element.18.refs_0_), channel_id=1, source_target_pairs={{0,1},{1,0},{2,3},{3,2},{4,5},{5,4},{6,7},{7,6},{8,9},{9,8},{10,11... | collective-permute-start | bytes 700424 | tf_op jit(solution)/shard_map/ppermute | solution.py:39
  22.3 1.4 %collective-permute-start.3 = (f32[11,24,128]{2,1,0:T(8,128)S(1)}, f32[11,24,128]{2,1,0:T(8,128)S(1)}, u32[]{:S(2)}, u32[]{:S(2)}) collective-permute-start(f32[11,24,128]{2,1,0:T(8,128)S(1)} %collective-permute-done.refs_1_), channel_id=1, source_target_pairs={{0,1},{1,0},{2,3},{3,2},{4,5},{5,4},{6,7},{7,6},{8,9},{9,8},{10,11... | collective-permute-start | bytes 405512 | tf_op jit(solution)/shard_map/ppermute | solution.py:39
  22.3 1.5 %collective-permute-start.4 = (f32[11,24,128]{2,1,0:T(8,128)S(1)}, f32[11,24,128]{2,1,0:T(8,128)S(1)}, u32[]{:S(2)}, u32[]{:S(2)}) collective-permute-start(f32[11,24,128]{2,1,0:T(8,128)S(1)} %collective-permute-done.1.refs_2_), channel_id=1, source_target_pairs={{0,1},{1,0},{2,3},{3,2},{4,5},{5,4},{6,7},{7,6},{8,9},{9,8},{10,11... | collective-permute-start | bytes 405512 | tf_op jit(solution)/shard_map/ppermute | solution.py:39
  24.3 12.8 %collective-permute-start.5 = (bf16[6,16,128]{2,1,0:T(8,128)(2,1)S(1)}, bf16[6,16,128]{2,1,0:T(8,128)(2,1)S(1)}, u32[]{:S(2)}, u32[]{:S(2)}) collective-permute-start(bf16[6,16,128]{2,1,0:T(8,128)(2,1)S(1)} %get-tuple-element.22), channel_id=1, source_target_pairs={{0,2},{2,4},{4,6},{6,8},{8,10},{10,12},{12,14},{14,16},{16,18},{18... | collective-permute-start | bytes 73736 | tf_op jit(solution)/shard_map/ppermute | solution.py:39
  25.7 11.5 %collective-permute-start.6 = (bf16[6,16,128]{2,1,0:T(8,128)(2,1)S(1)}, bf16[6,16,128]{2,1,0:T(8,128)(2,1)S(1)}, u32[]{:S(2)}, u32[]{:S(2)}) collective-permute-start(bf16[6,16,128]{2,1,0:T(8,128)(2,1)S(1)} %get-tuple-element.23), channel_id=1, source_target_pairs={{0,30},{2,0},{4,2},{6,4},{8,6},{10,8},{12,10},{14,12},{16,14},{18,... | collective-permute-start | bytes 73736 | tf_op jit(solution)/shard_map/ppermute | solution.py:39
